TPU v7x, 16 devices: a 4x2x1 block of a 4x4x8 slice. The times are simulated.
16 devices in a mesh: rep: 2 (over y, z), dp: 8 (over x, core).
Axes of the slice: x: 4, y: 2, z: 1, core: 2. Of those that a mesh axis runs over, the one named last changes fastest.
The devices are a block of a 4x4x8 slice.
Arguments:
- g_w_gate: bfloat16 [16, 2, 1024, 3328], P(('rep', 'dp')), parts along dimension 0
- g_w_up: bfloat16 [16, 2, 1024, 3328], P(('rep', 'dp')), parts along dimension 0
- g_w_down: bfloat16 [16, 2, 3328, 1024], P(('rep', 'dp')), parts along dimension 0
- w_gate: bfloat16 [2, 1024, 3328], replicated
- w_up: bfloat16 [2, 1024, 3328], replicated
- w_down: bfloat16 [2, 3328, 1024], replicated
- m_w_gate: float32 [2, 1024, 3328], P(None, 'dp')
- m_w_up: float32 [2, 1024, 3328], P(None, 'dp')
- m_w_down: float32 [2, 3328, 1024], P(None, 'dp')
- v_w_gate: float32 [2, 1024, 3328], P(None, 'dp')
- v_w_up: float32 [2, 1024, 3328], P(None, 'dp')
- v_w_down: float32 [2, 3328, 1024], P(None, 'dp')
Outputs:
- output 1: bfloat16 [4, 1024, 3328], P('rep'), parts along dimension 0
- output 2: bfloat16 [4, 1024, 3328], P('rep'), parts along dimension 0
- output 3: bfloat16 [4, 3328, 1024], P('rep'), parts along dimension 0
- output 4: float32 [4, 1024, 3328], P('rep', 'dp'), parts along dimension 0
- output 5: float32 [4, 1024, 3328], P('rep', 'dp'), parts along dimension 0
- output 6: float32 [4, 3328, 1024], P('rep', 'dp'), parts along dimension 0
- output 7: float32 [4, 1024, 3328], P('rep', 'dp'), parts along dimension 0
- output 8: float32 [4, 1024, 3328], P('rep', 'dp'), parts along dimension 0
- output 9: float32 [4, 3328, 1024], P('rep', 'dp'), parts along dimension 0
There are 2 independent parts. A program takes and returns all parts, laid end to end along the dimension named above; an argument that names none is the same for every part.
All inputs are finite; a program needn't handle non-finite values.
Results may differ from a plain program's by a relative error of at most 0.022.
Values are sent between devices in bfloat16 or wider.
A program may use at most 768 MiB of HBM per device.

v0:
```python
import jax
import jax.numpy as jnp
from jax import lax
from jax.sharding import PartitionSpec as P


def adamw(w, m, v, g):
    m = 0.9 * m + 0.1 * g
    v = 0.95 * v + 0.05 * g * g
    step = m * lax.rsqrt(v + 1e-8) + 0.1 * w
    return (w - 0.02 * step).astype(jnp.bfloat16), m, v


def solution(mesh):
    def step(*arrays):
        terms, weights, m, v = (arrays[i : i + 3] for i in (0, 3, 6, 9))
        gradients = [lax.psum_scatter(t[0], "dp", scatter_dimension=1, tiled=True).astype(jnp.float32) for t in terms]
        me = lax.axis_index("dp")
        own = [lax.dynamic_slice_in_dim(w, me * one.shape[1], one.shape[1], 1).astype(jnp.float32) for w, one in zip(weights, m, strict=True)]
        new = [adamw(w, m, v, g) for w, m, v, g in zip(own, m, v, gradients, strict=True)]
        whole = [lax.all_gather(one[0], "dp", axis=1, tiled=True) for one in new]
        return (*whole, *(one[1] for one in new), *(one[2] for one in new))

    all_of, cut = P(None, None, None), P(None, "dp", None)
    return jax.shard_map(
        step,
        mesh=mesh,
        in_specs=(P(("rep", "dp"), None, None, None),) * 3 + (all_of,) * 3 + (cut,) * 6,
        out_specs=(P("rep", None, None),) * 3 + (P("rep", "dp", None),) * 6,
        check_vma=False,
    )
```

profile of v0, /device:TPU:113, one launch (start us, length us, event | category | flops | bytes accessed | tf_op | source)
XLA Modules:
  0.0 481.7 jit_solution(6676009668953177155)
XLA Ops:
  7.2 0.1 reduce-scatter.8.cloned.1.call-start
  7.3 0.7 reduce-scatter.8.cloned.1.call-update
  8.0 0.1 reduce-scatter.6.cloned.1.call-start
  8.1 0.7 reduce-scatter.6.cloned.1.call-update
  8.8 0.1 reduce-scatter.4.cloned.1.call-start
  8.9 0.0 copy-start.1
  8.9 0.7 reduce-scatter.4.cloned.1.call-update
  9.6 0.1 all-gather.8.cloned.1.call-start
  9.7 76.5 %reduce-scatter.8.cloned.1.call-done = bf16[2,416,1024]{2,1,0:T(8,128)(2,1)} async-done(((bf16[2,3328,1024]{2,1,0:T(8,128)(2,1)}), bf16[2,416,1024]{2,1,0:T(8,128)(2,1)}) %reduce-scatter.8.cloned.1.call-update) | async-done | bytes 1703952 | tf_op jit(solution)/shard_map/reduce_scatter | solution.py:17
  86.2 0.0 copy-done.1
  86.2 5.8 %fusion.10 = (bf16[2,416,1024]{2,1,0:T(8,128)(2,1)}, f32[2,416,1024]{2,1,0:T(8,128)}, f32[2,416,1024]{2,1,0:T(8,128)}) fusion(bf16[2,3328,1024]{2,1,0:T(8,128)(2,1)} %param.17, s32[]{:T(128)S(6)} %select_n.8, bf16[2,416,1024]{2,1,0:T(8,128)(2,1)} %reduce-scatter.8.cloned.1.call-done, f32[2,416,1024]{2,1,0:T(8,128)S(1)} %copy-done.1, f32[2,416,1024]{2,1,0:T(8,128)} %param.20), kind=kLoop, calls=%fused_computation.22 | loop fusion | flops 13631488 | bytes 18743300 | tf_op jit(solution)/shard_map/convert_element_type | solution.py:11
  92.0 0.1 all-gather.8.cloned.1.call-update
  92.1 0.1 all-gather.6.cloned.1.call-start
  92.2 69.4 %reduce-scatter.6.cloned.1.call-done = bf16[2,128,3328]{2,1,0:T(8,128)(2,1)} async-done(((bf16[2,1024,3328]{2,1,0:T(8,128)(2,1)}), bf16[2,128,3328]{2,1,0:T(8,128)(2,1)}) %reduce-scatter.6.cloned.1.call-update) | async-done | bytes 1703952 | tf_op jit(solution)/shard_map/reduce_scatter | solution.py:17
  161.6 0.0 copy-start.2
  161.6 6.9 %fusion.6 = (bf16[2,128,3328]{2,1,0:T(8,128)(2,1)}, f32[2,128,3328]{2,1,0:T(8,128)}, f32[2,128,3328]{2,1,0:T(8,128)}) fusion(bf16[2,1024,3328]{2,1,0:T(8,128)(2,1)} %param.16, s32[]{:T(128)S(6)} %select_n.7, bf16[2,128,3328]{2,1,0:T(8,128)(2,1)} %reduce-scatter.6.cloned.1.call-done, f32[2,128,3328]{2,1,0:T(8,128)} %param.22, f32[2,128,3328]{2,1,0:T(8,128)} %param.19), kind=kLoop, calls=%fused_computation.18 | loop fusion | flops 13631488 | bytes 18743300 | tf_op jit(solution)/shard_map/convert_element_type | solution.py:11
  168.5 0.1 all-gather.6.cloned.1.call-update
  168.5 0.1 all-gather.4.cloned.1.call-start
  168.6 68.3 %reduce-scatter.4.cloned.1.call-done = bf16[2,128,3328]{2,1,0:T(8,128)(2,1)} async-done(((bf16[2,1024,3328]{2,1,0:T(8,128)(2,1)}), bf16[2,128,3328]{2,1,0:T(8,128)(2,1)}) %reduce-scatter.4.cloned.1.call-update) | async-done | bytes 1703952 | tf_op jit(solution)/shard_map/reduce_scatter | solution.py:17
  236.9 0.0 copy-done.2
  236.9 5.7 %fusion.2 = (bf16[2,128,3328]{2,1,0:T(8,128)(2,1)}, f32[2,128,3328]{2,1,0:T(8,128)}, f32[2,128,3328]{2,1,0:T(8,128)}) fusion(bf16[2,1024,3328]{2,1,0:T(8,128)(2,1)} %param.15, s32[]{:T(128)S(6)} %select_n.7, bf16[2,128,3328]{2,1,0:T(8,128)(2,1)} %reduce-scatter.4.cloned.1.call-done, f32[2,128,3328]{2,1,0:T(8,128)S(1)} %copy-done.2, f32[2,128,3328]{2,1,0:T(8,128)} %param.18), kind=kLoop, calls=%fused_computation.14 | loop fusion | flops 13631488 | bytes 18743300 | tf_op jit(solution)/shard_map/convert_element_type | solution.py:11
  242.7 0.1 all-gather.4.cloned.1.call-update
  242.7 64.5 %all-gather.8.cloned.1.call-done = bf16[2,3328,1024]{2,1,0:T(8,128)(2,1)} async-done(((bf16[2,416,1024]{2,1,0:T(8,128)(2,1)}), bf16[2,3328,1024]{2,1,0:T(8,128)(2,1)}) %all-gather.8.cloned.1.call-update) | async-done | bytes 13631504 | tf_op jit(solution)/shard_map/all_gather | solution.py:21
  307.2 70.2 %all-gather.6.cloned.1.call-done = bf16[2,1024,3328]{2,1,0:T(8,128)(2,1)} async-done(((bf16[2,128,3328]{2,1,0:T(8,128)(2,1)}), bf16[2,1024,3328]{2,1,0:T(8,128)(2,1)}) %all-gather.6.cloned.1.call-update) | async-done | bytes 13631504 | tf_op jit(solution)/shard_map/all_gather | solution.py:21
  377.4 70.2 %all-gather.4.cloned.1.call-done = bf16[2,1024,3328]{2,1,0:T(8,128)(2,1)} async-done(((bf16[2,128,3328]{2,1,0:T(8,128)(2,1)}), bf16[2,1024,3328]{2,1,0:T(8,128)(2,1)}) %all-gather.4.cloned.1.call-update) | async-done | bytes 13631504 | tf_op jit(solution)/shard_map/all_gather | solution.py:21
  447.5 0.0 copy-start
  447.5 0.0 slice-start
  447.5 0.0 slice-start.1
  447.5 15.1 %copy.24 = bf16[2,1024,3328]{2,1,0:T(8,128)(2,1)} copy(bf16[2,1024,3328]{2,1,0:T(8,128)(2,1)} %all-gather.4.cloned.1.call-done) | data formatting | bytes 27262976
  462.6 0.0 copy-done
  462.6 0.0 slice-start.2
  462.6 0.0 slice-start.3
  462.6 6.6 %copy.25 = bf16[2,1024,3328]{2,1,0:T(8,128)(2,1)} copy(bf16[2,1024,3328]{2,1,0:T(8,128)(2,1)S(1)} %copy-done) | data formatting | bytes 27262976
  469.2 0.0 slice-done
  469.2 0.0 slice-done.1
  469.2 0.0 slice-done.2
  469.2 0.5 slice-done.3
  469.7 5.1 %copy.26 = bf16[2,3328,1024]{2,1,0:T(8,128)(2,1)} copy(bf16[2,3328,1024]{2,1,0:T(8,128)(2,1)S(1)} %bitcast.7) | data formatting | bytes 27262976
  (1 shorter events, 0.0 us)
Async XLA Ops:
  7.2 79.0 %reduce-scatter.8.cloned.1.call-start = ((), (), s32[]{:S(2)}) async-start(), calls=%async_computation.7 | async-start | bytes 15335424 | tf_op jit(solution)/shard_map/reduce_scatter | solution.py:17
  8.0 153.6 %reduce-scatter.6.cloned.1.call-start = ((), (), s32[]{:S(2)}) async-start(), calls=%async_computation.5 | async-start | bytes 15335424 | tf_op jit(solution)/shard_map/reduce_scatter | solution.py:17
  8.8 228.1 %reduce-scatter.4.cloned.1.call-start = ((), (), s32[]{:S(2)}) async-start(), calls=%async_computation.3 | async-start | bytes 15335424 | tf_op jit(solution)/shard_map/reduce_scatter | solution.py:17
  8.9 77.3 %copy-start.1 = (f32[2,416,1024]{2,1,0:T(8,128)S(1)}, f32[2,416,1024]{2,1,0:T(8,128)}, u32[]{:S(2)}) copy-start(f32[2,416,1024]{2,1,0:T(8,128)} %param.23) | copy-start | bytes 10223620
  9.6 297.6 %all-gather.8.cloned.1.call-start = ((), (), s32[]{:S(2)}) async-start(), calls=%async_computation.8 | async-start | bytes 15335424 | tf_op jit(solution)/shard_map/all_gather | solution.py:21
  92.1 285.3 %all-gather.6.cloned.1.call-start = ((), (), s32[]{:S(2)}) async-start(), calls=%async_computation.6 | async-start | bytes 15335424 | tf_op jit(solution)/shard_map/all_gather | solution.py:21
  161.6 75.4 %copy-start.2 = (f32[2,128,3328]{2,1,0:T(8,128)S(1)}, f32[2,128,3328]{2,1,0:T(8,128)}, u32[]{:S(2)}) copy-start(f32[2,128,3328]{2,1,0:T(8,128)} %param.21) | copy-start | bytes 10223620
  168.5 279.0 %all-gather.4.cloned.1.call-start = ((), (), s32[]{:S(2)}) async-start(), calls=%async_computation.4 | async-start | bytes 15335424 | tf_op jit(solution)/shard_map/all_gather | solution.py:21
  447.5 15.1 %copy-start = (bf16[2,1024,3328]{2,1,0:T(8,128)(2,1)S(1)}, bf16[2,1024,3328]{2,1,0:T(8,128)(2,1)}, u32[]{:S(2)}) copy-start(bf16[2,1024,3328]{2,1,0:T(8,128)(2,1)} %all-gather.6.cloned.1.call-done) | copy-start | bytes 40894468
  447.5 21.6 %slice-start = ((s8[13631488]{0:T(1024)(128)(4,1)}), s8[4194304]{0:T(1024)(128)(4,1)S(1)}, s32[]{:S(2)}) async-start(s8[13631488]{0:T(1024)(128)(4,1)} %bitcast.6), calls=%async_computation.9 | async-start | bytes 8388608
  447.5 21.6 %slice-start.1 = ((s8[13631488]{0:T(1024)(128)(4,1)}), s8[4194304]{0:T(1024)(128)(4,1)S(1)}, s32[]{:S(2)}) async-start(s8[13631488]{0:T(1024)(128)(4,1)} %bitcast.6), calls=%async_computation.10 | async-start | bytes 8388608
  462.6 6.6 %slice-start.2 = ((s8[13631488]{0:T(1024)(128)(4,1)}), s8[4194304]{0:T(1024)(128)(4,1)S(1)}, s32[]{:S(2)}) async-start(s8[13631488]{0:T(1024)(128)(4,1)} %bitcast.6), calls=%async_computation.11 | async-start | bytes 8388608
  462.6 7.1 %slice-start.3 = ((s8[13631488]{0:T(1024)(128)(4,1)}), s8[1048576]{0:T(1024)(128)(4,1)S(1)}, s32[]{:S(2)}) async-start(s8[13631488]{0:T(1024)(128)(4,1)} %bitcast.6), calls=%async_computation.12 | async-start | bytes 2097152
Sparse Core Ops, SparseCore 0:
  10.3 75.8 reduce-scatter.7
  88.5 73.0 reduce-scatter.5
  163.9 73.0 reduce-scatter.3
  238.9 68.2 all-gather.7
  309.2 68.1 all-gather.5
  379.4 68.1 all-gather.3
where the time goes:
time: 482 us
  waiting for transfers between devices  421 us (87%)
  local copies, waits for them, and re-layouts  27.3 us (6%)
  other arithmetic  18.5 us (4%)
  between operations  14.2 us (3%)
    reduce_scatter x3, waiting for transfers between devices, step(): lax.psum_scatter(t[0], 'dp', scatter_dimension=1, tiled=True)  214 us
    all_gather x3, waiting for transfers between devices, step(): whole = [lax.all_gather(one[0], 'dp', axis=1, tiled=True) for one in new]  205 us
    unnamed x17, local copies, waits for them, and re-layouts  27.3 us
    convert_element_type x3, other arithmetic, adamw(): return ((w - 0.02 * step).astype(jnp.bfloat16), m, v)  18.5 us
  transfers between devices with their start and end apart: 6, of which 6 were waited for; matrix products, arithmetic and copies ran while one was open for 4% of the time, Pallas kernels for 0%

commit v1 on v0

v1 whole, which is shorter than its diff:
```python
import functools

import jax
import jax.numpy as jnp
from jax import lax
from jax.experimental import pallas as pl
from jax.experimental.pallas import tpu as pltpu
from jax.sharding import PartitionSpec as P

MESH = pl.DeviceIdType.MESH
CORES = 2
STRIP = 16
SLOTS = 6
SETS = 3


def f32(x):
    return x.astype(jnp.float32)


def strips(rows, body):
    def one(i, carry):
        body(pl.ds(pl.multiple_of(i * STRIP, STRIP), STRIP))
        return carry

    lax.fori_loop(0, rows // STRIP, one, None)


def kernel(chips, layers, kinds, *refs):
    count = len(kinds)
    take = iter(refs)
    g, w, m, v, w_out, m_out, v_out, part, arrived = ([next(take) for _ in range(count)] for _ in range(9))
    shapes = max(kinds) + 1
    own, m_set, v_set, w_set = ([next(take) for _ in range(shapes)] for _ in range(4))
    own_sem, set_in, set_out, pair_send, pair_recv, ring_send, ring_recv, gather_send, gather_recv, local_sem = take

    me = lax.axis_index("dp")
    chip, core = me // CORES, me % CORES
    partner = chip * CORES + (1 - core)
    turn = [lax.rem(chip + d, chips) for d in range(chips)]
    right, left = turn[1] * CORES + core, turn[chips - 1] * CORES + core
    far = chips // 2

    chunks = [(a, layer) for a in range(count) for layer in range(layers)]
    rows = [r.shape[2] for r in part]
    half = [r // 2 for r in rows]

    barrier = pltpu.get_barrier_semaphore()
    for other in (partner, right, left):
        pl.semaphore_signal(barrier, inc=1, device_id={"dp": other}, device_id_type=MESH)
    pl.semaphore_wait(barrier, 3)

    def remote(src, dst, send, recv, to):
        return pltpu.make_async_remote_copy(src_ref=src, dst_ref=dst, send_sem=send, recv_sem=recv, device_id={"dp": to}, device_id_type=MESH)

    waits = []

    order = (far, 1, chips - 1, 0)

    def pair_copy(j, n):
        a, layer = chunks[j]
        d = order[n]
        src = g[a].at[0, layer, pl.ds(pl.multiple_of((turn[d] * CORES + 1 - core) * rows[a], STRIP), rows[a])]
        s = j * chips + n
        return remote(src, part[a].at[layer, d], pair_send.at[s], pair_recv.at[s], partner)

    def start_pair(j):
        for n in range(chips):
            copy = pair_copy(j, n)
            copy.start()
            waits.append(copy.wait_send)

    seen = set()

    def need_pair(j, d):
        if (j, d) not in seen:
            seen.add((j, d))
            pair_copy(j, order.index(d)).wait_recv()

    uses = []
    for s in range(len(chunks) + 2):
        if s < len(chunks):
            uses += [(s, far, 0), (s, far, 1), (s, 1, 1), (s, chips - 1, 0)]
        if 0 <= s - 1 < len(chunks):
            uses += [(s - 1, 1, 0), (s - 1, chips - 1, 1)]
        if 0 <= s - 2 < len(chunks):
            uses += [(s - 2, 0, 0), (s - 2, 0, 1)]
    of_kind = [[u for u in uses if kinds[chunks[u[0]][0]] == q] for q in range(shapes)]

    def own_copy(q, i):
        j, d, h = of_kind[q][i]
        a, layer = chunks[j]
        src = g[a].at[0, layer, pl.ds(pl.multiple_of((turn[d] * CORES + core) * rows[a] + h * half[a], STRIP), half[a])]
        return pltpu.make_async_copy(src, own[q].at[i % SLOTS], own_sem.at[q, i % SLOTS])

    for q in range(shapes):
        for i in range(min(SLOTS, len(of_kind[q]))):
            own_copy(q, i).start()
    used = [0] * shapes

    def add_own(j, d, h, extra, finish=None):
        a, layer = chunks[j]
        q = kinds[a]
        i = used[q]
        used[q] += 1
        assert of_kind[q][i] == (j, d, h)
        need_pair(j, d)
        own_copy(q, i).wait()
        mine = own[q].at[i % SLOTS]
        total = part[a].at[layer, d, pl.ds(h * half[a], half[a])]

        def body(strip):
            x = f32(total[strip, :]) + f32(mine[strip, :])
            for one in extra:
                x = x + f32(one[strip, :])
            x = x.astype(jnp.bfloat16)
            total[strip, :] = x if finish is None else finish(strip, f32(x))

        strips(half[a], body)
        if i + SLOTS < len(of_kind[q]):
            own_copy(q, i + SLOTS).start()
        return total

    def ring_copy(j, slot):
        a, layer = chunks[j]
        d, h = ((far, 0), (1, 1), (1, 0), (far, 1), (chips - 1, 0), (chips - 1, 1))[slot]
        src = part[a].at[layer, d, pl.ds(h * half[a], half[a])]
        s = j * 6 + slot
        return remote(src, arrived[a].at[layer, slot], ring_send.at[s], ring_recv.at[s], right if slot < 3 else left)

    def send(j, slot):
        copy = ring_copy(j, slot)
        copy.start()
        waits.append(copy.wait_send)

    def arrival(j, slot):
        ring_copy(j, slot).wait_recv()
        a, layer = chunks[j]
        return arrived[a].at[layer, slot]

    def first(j):
        add_own(j, far, 0, ())
        send(j, 0)
        add_own(j, far, 1, ())
        send(j, 3)
        add_own(j, 1, 1, ())
        send(j, 1)
        add_own(j, chips - 1, 0, ())
        send(j, 4)

    def middle(j):
        add_own(j, 1, 0, (arrival(j, 0),))
        send(j, 2)
        add_own(j, chips - 1, 1, (arrival(j, 3),))
        send(j, 5)

    units = [[(j, h) for j in range(len(chunks)) for h in range(2) if kinds[chunks[j][0]] == q] for q in range(shapes)]

    def set_copies(q, i):
        j, h = units[q][i]
        a, layer = chunks[j]
        cut = pl.ds(h * half[a], half[a])
        mine = pl.ds(pl.multiple_of(me * rows[a] + h * half[a], STRIP), half[a])
        t = i % SETS
        return [
            pltpu.make_async_copy(m[a].at[layer, cut], m_set[q].at[t], set_in.at[q, t, 0]),
            pltpu.make_async_copy(v[a].at[layer, cut], v_set[q].at[t], set_in.at[q, t, 1]),
            pltpu.make_async_copy(w[a].at[layer, mine], w_set[q].at[t], set_in.at[q, t, 2]),
        ], [
            pltpu.make_async_copy(m_set[q].at[t], m_out[a].at[layer, cut], set_out.at[q, t, 0]),
            pltpu.make_async_copy(v_set[q].at[t], v_out[a].at[layer, cut], set_out.at[q, t, 1]),
        ]

    def start_set(q, i):
        if i < len(units[q]):
            if i >= SETS:
                for copy in set_copies(q, i - SETS)[1]:
                    copy.wait()
            for copy in set_copies(q, i)[0]:
                copy.start()

    for q in range(shapes):
        for i in range(SETS - 1):
            start_set(q, i)

    def update(j, h, extra):
        a, layer = chunks[j]
        q = kinds[a]
        i = units[q].index((j, h))
        ins, outs = set_copies(q, i)
        for copy in ins:
            copy.wait()
        mm, vv, ww = (s[q].at[i % SETS] for s in (m_set, v_set, w_set))

        def finish(strip, grad):
            old = f32(ww[strip, :])
            new_m = 0.9 * mm[strip, :] + 0.1 * grad
            new_v = 0.95 * vv[strip, :] + 0.05 * grad * grad
            mm[strip, :] = new_m
            vv[strip, :] = new_v
            step = new_m * lax.rsqrt(new_v + 1e-8) + 0.1 * old
            return (old - 0.02 * step).astype(jnp.bfloat16)

        add_own(j, 0, h, extra, finish)
        for copy in outs:
            copy.start()
        start_set(q, i + SETS - 1)

    def block(a, layer, chip_of, core_of, h=None):
        base = (chip_of * CORES + core_of) * rows[a]
        if h is None:
            return w_out[a].at[layer, pl.ds(pl.multiple_of(base, STRIP), rows[a])]
        return w_out[a].at[layer, pl.ds(pl.multiple_of(base + h * half[a], STRIP), half[a])]

    def gather_copy(j, n):
        a, layer = chunks[j]
        s = (gather_send.at[j, n], gather_recv.at[j, n])
        mine = lambda h: part[a].at[layer, 0, pl.ds(h * half[a], half[a])]
        if n < 4:
            h, to = n % 2, right if n < 2 else left
            return remote(mine(h), block(a, layer, chip, core, h), *s, to)
        if n < 6:
            d, h, to = ((chips - 1, 0, right), (1, 1, left))[n - 4]
            there = block(a, layer, turn[d], core, h)
            return remote(there, there, *s, to)
        if n == 6:
            return remote(part[a].at[layer, 0], block(a, layer, chip, core), *s, partner)
        d, h = ((chips - 1, None), (1, None), (far, 0), (far, 1))[n - 7]
        there = block(a, layer, turn[d], core, h)
        return remote(there, there, *s, partner)

    def go(j, n):
        copy = gather_copy(j, n)
        copy.start()
        waits.append(copy.wait_send)
        if n >= 6:
            waits.append(copy.wait_recv)

    def final(j):
        a, layer = chunks[j]
        update(j, 0, (arrival(j, 2), arrival(j, 4)))
        go(j, 0)
        update(j, 1, (arrival(j, 1), arrival(j, 5)))
        go(j, 3)
        go(j, 1)
        go(j, 2)
        go(j, 6)
        keep = pltpu.make_async_copy(part[a].at[layer, 0], block(a, layer, chip, core), local_sem.at[j])
        keep.start()
        waits.append(keep.wait)

    def pass_on(j):
        gather_copy(j, 0).wait_recv()
        go(j, 4)
        gather_copy(j, 3).wait_recv()
        go(j, 5)
        gather_copy(j, 1).wait_recv()
        go(j, 7)
        gather_copy(j, 2).wait_recv()
        go(j, 8)

    def hand_over(j):
        gather_copy(j, 4).wait_recv()
        go(j, 9)
        gather_copy(j, 5).wait_recv()
        go(j, 10)

    total = len(chunks)
    start_pair(0)
    for s in range(total + 5):
        if s + 1 < total:
            start_pair(s + 1)
        for back, act in ((0, first), (1, middle), (2, final), (4, pass_on), (5, hand_over)):
            if 0 <= s - back < total:
                act(s - back)

    for q in range(shapes):
        for i in range(max(0, len(units[q]) - SETS), len(units[q])):
            for copy in set_copies(q, i)[1]:
                copy.wait()
    for wait in waits:
        wait()


def solution(mesh):
    devices = mesh.shape["dp"]
    chips = devices // CORES

    def step(*arrays):
        terms, weights, m, v = (arrays[i : i + 3] for i in (0, 3, 6, 9))
        count, layers = len(weights), weights[0].shape[0]
        blocks = [one.shape[1:] for one in m]
        distinct = list(dict.fromkeys(blocks))
        kinds = tuple(distinct.index(b) for b in blocks)
        chunks = count * layers
        any_space = pl.BlockSpec(memory_space=pl.ANY)
        bf16 = jnp.bfloat16
        halves = [(b[0] // 2, b[1]) for b in distinct]
        dma = pltpu.SemaphoreType.DMA
        out = pl.pallas_call(
            functools.partial(kernel, chips, layers, kinds),
            out_shape=[jax.ShapeDtypeStruct(one.shape, one.dtype) for one in (*weights, *m, *v)],
            in_specs=[any_space] * 4 * count,
            out_specs=[any_space] * 3 * count,
            scratch_shapes=[pltpu.VMEM((layers, chips, *b), bf16) for b in blocks]
            + [pltpu.VMEM((layers, 6, b[0] // 2, b[1]), bf16) for b in blocks]
            + [pltpu.VMEM((SLOTS, *b), bf16) for b in halves]
            + [pltpu.VMEM((SETS, *b), jnp.float32) for b in halves] * 2
            + [pltpu.VMEM((SETS, *b), bf16) for b in halves]
            + [dma((len(distinct), SLOTS)), dma((len(distinct), SETS, 3)), dma((len(distinct), SETS, 2))]
            + [dma((chunks * chips,))] * 2
            + [dma((chunks * 6,))] * 2
            + [dma((chunks, 11))] * 2
            + [dma((chunks,))],
            compiler_params=pltpu.CompilerParams(collective_id=0, has_side_effects=True, vmem_limit_bytes=62 * 1024 * 1024),
        )(*terms, *weights, *m, *v)
        return tuple(out)

    all_of, cut = P(None, None, None), P(None, "dp", None)
    return jax.shard_map(
        step,
        mesh=mesh,
        in_specs=(P(("rep", "dp"), None, None, None),) * 3 + (all_of,) * 3 + (cut,) * 6,
        out_specs=(P("rep", None, None),) * 3 + (P("rep", "dp", None),) * 6,
        check_vma=False,
    )
```

time: 482 us -> 388 us (0.80)
  waiting for transfers between devices: 421 us -> 0 us
  Pallas kernels: 0 us -> 342 us
  other arithmetic: 18.5 us -> 0.01 us
  local copies, waits for them, and re-layouts: 27.3 us -> 45.5 us
  between operations: 14.2 us -> 0.7 us
    pallas_call x0 -> x1, Pallas kernels: none -> 342 us  [step(): pl.pallas_call(functools.partial(kernel, chips, layers, kinds), out_shape...]
    reduce_scatter x3 -> x0, waiting for transfers between devices: 214 us -> none  [step(): lax.psum_scatter(t[0], 'dp', scatter_dimension=1, tiled=True)]
    all_gather x3 -> x0, waiting for transfers between devices: 205 us -> none  [step(): whole = [lax.all_gather(one[0], 'dp', axis=1, tiled=True) for one in new]]
    convert_element_type x3 -> x0, other arithmetic: 18.5 us -> none  [adamw(): return ((w - 0.02 * step).astype(jnp.bfloat16), m, v)]
    unnamed x17 -> x31, local copies, waits for them, and re-layouts: 27.3 us -> 45.5 us
  transfers between devices with their start and end apart: 6 -> 0, of which waited for: 6 -> 0; matrix products, arithmetic and copies ran while one was open for 4% -> 0% of each run, Pallas kernels for 0% -> 0%
where the time goes in v1:
time: 388 us
  Pallas kernels  342 us (88%)
  local copies, waits for them, and re-layouts  45.5 us (12%)
    pallas_call x1, Pallas kernels, step(): pl.pallas_call(functools.partial(kernel, chips, layers, kinds), out_shape...  342 us
    unnamed x31, local copies, waits for them, and re-layouts  45.5 us

profile of v1, /device:TPU:113, one launch (start us, length us, event | category | flops | bytes accessed | tf_op | source)
XLA Modules:
  0.0 388.0 jit_solution(3181377413646599681)
XLA Ops:
  0.6 341.8 %shard_map.187 = (bf16[2,1024,3328]{2,1,0:T(8,128)(2,1)}, bf16[2,1024,3328]{2,1,0:T(8,128)(2,1)}, bf16[2,3328,1024]{2,1,0:T(8,128)(2,1)}, f32[2,128,3328]{2,1,0:...) custom-call(bf16[1,2,1024,3328]{3,2,1,0:T(8,128)(2,1)} %refs_0_.1, ...), custom_call_target="tpu_custom_call" | custom-call | tf_op jit(solution)/shard_map/pallas_call | solution.py:300
  342.5 0.0 copy-start
  342.5 0.0 slice-start
  342.5 0.0 slice-start.1
  342.5 0.0 slice-start.2
  342.5 15.1 %copy.30 = bf16[2,1024,3328]{2,1,0:T(8,128)(2,1)} copy(bf16[2,1024,3328]{2,1,0:T(8,128)(2,1)} %get-tuple-element.18) | data formatting | bytes 27262976
  357.6 0.0 copy-done
  357.6 0.0 slice-start.3
  357.6 6.5 %copy.31 = bf16[2,1024,3328]{2,1,0:T(8,128)(2,1)} copy(bf16[2,1024,3328]{2,1,0:T(8,128)(2,1)S(1)} %copy-done) | data formatting | bytes 27262976
  364.1 0.0 slice-done
  364.1 0.0 slice-done.1
  364.1 0.0 slice-done.2
  364.1 0.4 slice-done.3
  364.6 0.0 copy-start.6
  364.6 5.7 %copy.32 = bf16[2,3328,1024]{2,1,0:T(8,128)(2,1)} copy(bf16[2,3328,1024]{2,1,0:T(8,128)(2,1)S(1)} %bitcast.1) | data formatting | bytes 27262976
  370.3 0.0 copy-done.6
  370.3 0.0 copy-start.5
  370.3 1.8 copy.33
  372.1 1.4 copy-done.5
  373.5 0.0 copy-start.4
  373.5 1.7 copy.34
  375.3 1.4 copy-done.4
  376.7 0.0 copy-start.3
  376.7 1.7 copy.35
  378.5 1.4 copy-done.3
  379.9 0.0 copy-start.2
  379.9 1.7 copy.36
  381.7 1.4 copy-done.2
  383.1 0.0 copy-start.1
  383.1 1.7 copy.37
  384.8 1.4 copy-done.1
  386.3 1.7 copy.38
  (1 shorter events, 0.0 us)
Async XLA Ops:
  342.5 15.1 %copy-start = (bf16[2,1024,3328]{2,1,0:T(8,128)(2,1)S(1)}, bf16[2,1024,3328]{2,1,0:T(8,128)(2,1)}, u32[]{:S(2)}) copy-start(bf16[2,1024,3328]{2,1,0:T(8,128)(2,1)} %get-tuple-element.19) | copy-start | bytes 40894468
  342.5 21.6 %slice-start = ((s8[13631488]{0:T(1024)(128)(4,1)}), s8[4194304]{0:T(1024)(128)(4,1)S(1)}, s32[]{:S(2)}) async-start(s8[13631488]{0:T(1024)(128)(4,1)} %bitcast), calls=%async_computation | async-start | bytes 8388608
  342.5 21.6 %slice-start.1 = ((s8[13631488]{0:T(1024)(128)(4,1)}), s8[4194304]{0:T(1024)(128)(4,1)S(1)}, s32[]{:S(2)}) async-start(s8[13631488]{0:T(1024)(128)(4,1)} %bitcast), calls=%async_computation.1 | async-start | bytes 8388608
  342.5 21.6 %slice-start.2 = ((s8[13631488]{0:T(1024)(128)(4,1)}), s8[4194304]{0:T(1024)(128)(4,1)S(1)}, s32[]{:S(2)}) async-start(s8[13631488]{0:T(1024)(128)(4,1)} %bitcast), calls=%async_computation.2 | async-start | bytes 8388608
  357.6 7.0 %slice-start.3 = ((s8[13631488]{0:T(1024)(128)(4,1)}), s8[1048576]{0:T(1024)(128)(4,1)S(1)}, s32[]{:S(2)}) async-start(s8[13631488]{0:T(1024)(128)(4,1)} %bitcast), calls=%async_computation.3 | async-start | bytes 2097152
  364.6 5.7 %copy-start.6 = (f32[2,128,3328]{2,1,0:T(8,128)S(1)}, f32[2,128,3328]{2,1,0:T(8,128)}, u32[]{:S(2)}) copy-start(f32[2,128,3328]{2,1,0:T(8,128)} %get-tuple-element.21) | copy-start | bytes 10223620
  370.3 3.2 copy-start.5
  373.5 3.2 copy-start.4
  376.7 3.2 copy-start.3
  379.9 3.2 copy-start.2
  383.1 3.2 copy-start.1

commit v2 on v1

--- a/solution.py
+++ b/solution.py
@@ -7,10 +7,12 @@
 from jax.experimental.pallas import tpu as pltpu
 from jax.sharding import PartitionSpec as P
 
+
 MESH = pl.DeviceIdType.MESH
 CORES = 2
 STRIP = 16
 SLOTS = 6
+VMEM = 67043328
 SETS = 3
 
 
@@ -28,8 +30,13 @@
 
 def kernel(chips, layers, kinds, *refs):
     count = len(kinds)
+    last = count - 1
     take = iter(refs)
-    g, w, m, v, w_out, m_out, v_out, part, arrived = ([next(take) for _ in range(count)] for _ in range(9))
+    g, w, m, v = ([next(take) for _ in range(count)] for _ in range(4))
+    w_out = [next(take) for _ in range(last)]
+    new_half = [next(take) for _ in range(2)]
+    new_pair = next(take)
+    m_out, v_out, part, arrived = ([next(take) for _ in range(count)] for _ in range(4))
     shapes = max(kinds) + 1
     own, m_set, v_set, w_set = ([next(take) for _ in range(shapes)] for _ in range(4))
     own_sem, set_in, set_out, pair_send, pair_recv, ring_send, ring_recv, gather_send, gather_recv, local_sem = take
@@ -45,46 +52,48 @@
     rows = [r.shape[2] for r in part]
     half = [r // 2 for r in rows]
 
-    barrier = pltpu.get_barrier_semaphore()
-    for other in (partner, right, left):
-        pl.semaphore_signal(barrier, inc=1, device_id={"dp": other}, device_id_type=MESH)
-    pl.semaphore_wait(barrier, 3)
-
     def remote(src, dst, send, recv, to):
         return pltpu.make_async_remote_copy(src_ref=src, dst_ref=dst, send_sem=send, recv_sem=recv, device_id={"dp": to}, device_id_type=MESH)
 
     waits = []
 
-    order = (far, 1, chips - 1, 0)
-
-    def pair_copy(j, n):
-        a, layer = chunks[j]
-        d = order[n]
-        src = g[a].at[0, layer, pl.ds(pl.multiple_of((turn[d] * CORES + 1 - core) * rows[a], STRIP), rows[a])]
-        s = j * chips + n
-        return remote(src, part[a].at[layer, d], pair_send.at[s], pair_recv.at[s], partner)
+    def finish_later(copy, *ends):
+        copy.start()
+        waits.extend(getattr(copy, end) for end in ends)
+
+    order = ((far, 0), (far, 1), (1, 1), (chips - 1, 0), (1, 0), (chips - 1, 1), (0, 0), (0, 1))
+
+    def pair_copy(j, d, h):
+        a, layer = chunks[j]
+        src = g[a].at[0, layer, pl.ds(pl.multiple_of((turn[d] * CORES + 1 - core) * rows[a] + h * half[a], STRIP), half[a])]
+        s = j * len(order) + order.index((d, h))
+        return remote(src, part[a].at[layer, d, pl.ds(h * half[a], half[a])], pair_send.at[s], pair_recv.at[s], partner)
 
     def start_pair(j):
-        for n in range(chips):
-            copy = pair_copy(j, n)
-            copy.start()
-            waits.append(copy.wait_send)
-
-    seen = set()
-
-    def need_pair(j, d):
-        if (j, d) not in seen:
-            seen.add((j, d))
-            pair_copy(j, order.index(d)).wait_recv()
+        for d, h in order:
+            finish_later(pair_copy(j, d, h), "wait_send")
+
+    total = len(chunks)
+    gathered = [j for j in range(total) if chunks[j][0] != last]
+    plan = [("pair", 0)]
+    for s in range(total):
+        plan += [("first", s)]
+        plan += [("pair", s + 1)] if s + 1 < total else []
+        plan += [("middle", s - 1)] if s >= 1 else []
+        plan += [("middle", s)] if s == total - 1 else []
+        plan += [("final", s - 2)] if s >= 2 else []
+        plan += [("pass", s - 4)] if s >= 4 else []
+        plan += [("hand", s - 5)] if s >= 5 else []
+    passed = [j for act, j in plan if act == "pass"]
+    handed = [j for act, j in plan if act == "hand"]
+    rest = [j for j in gathered if j not in passed]
+    plan += [("pass", rest[0]), ("final", total - 2)]
+    plan += [("pass", j) for j in rest[1:]] + [("final", total - 1)]
+    plan += [("hand", j) for j in gathered if j not in handed]
 
     uses = []
-    for s in range(len(chunks) + 2):
-        if s < len(chunks):
-            uses += [(s, far, 0), (s, far, 1), (s, 1, 1), (s, chips - 1, 0)]
-        if 0 <= s - 1 < len(chunks):
-            uses += [(s - 1, 1, 0), (s - 1, chips - 1, 1)]
-        if 0 <= s - 2 < len(chunks):
-            uses += [(s - 2, 0, 0), (s - 2, 0, 1)]
+    for act, j in plan:
+        uses += [(j, d, h) for d, h in {"first": order[:4], "middle": order[4:6], "final": order[6:]}.get(act, ())]
     of_kind = [[u for u in uses if kinds[chunks[u[0]][0]] == q] for q in range(shapes)]
 
     def own_copy(q, i):
@@ -104,7 +113,7 @@
         i = used[q]
         used[q] += 1
         assert of_kind[q][i] == (j, d, h)
-        need_pair(j, d)
+        pair_copy(j, d, h).wait_recv()
         own_copy(q, i).wait()
         mine = own[q].at[i % SLOTS]
         total = part[a].at[layer, d, pl.ds(h * half[a], half[a])]
@@ -129,9 +138,7 @@
         return remote(src, arrived[a].at[layer, slot], ring_send.at[s], ring_recv.at[s], right if slot < 3 else left)
 
     def send(j, slot):
-        copy = ring_copy(j, slot)
-        copy.start()
-        waits.append(copy.wait_send)
+        finish_later(ring_copy(j, slot), "wait_send")
 
     def arrival(j, slot):
         ring_copy(j, slot).wait_recv()
@@ -184,7 +191,7 @@
             start_set(q, i)
 
     def update(j, h, extra):
-        a, layer = chunks[j]
+        a, _ = chunks[j]
         q = kinds[a]
         i = units[q].index((j, h))
         ins, outs = set_copies(q, i)
@@ -230,14 +237,18 @@
         return remote(there, there, *s, partner)
 
     def go(j, n):
-        copy = gather_copy(j, n)
-        copy.start()
-        waits.append(copy.wait_send)
-        if n >= 6:
-            waits.append(copy.wait_recv)
+        finish_later(gather_copy(j, n), "wait_send", *(("wait_recv",) if n >= 6 else ()))
 
     def final(j):
         a, layer = chunks[j]
+        if a == last:
+            for h, slots in enumerate(((2, 4), (1, 5))):
+                update(j, h, [arrival(j, slot) for slot in slots])
+                half_of = part[a].at[layer, 0, pl.ds(h * half[a], half[a])]
+                finish_later(pltpu.make_async_copy(half_of, new_half[h].at[layer], local_sem.at[j, h]), "wait")
+            pair = remote(part[a].at[layer, 0], new_pair.at[layer], gather_send.at[j, 6], gather_recv.at[j, 6], partner)
+            finish_later(pair, "wait_send", "wait_recv")
+            return
         update(j, 0, (arrival(j, 2), arrival(j, 4)))
         go(j, 0)
         update(j, 1, (arrival(j, 1), arrival(j, 5)))
@@ -245,9 +256,7 @@
         go(j, 1)
         go(j, 2)
         go(j, 6)
-        keep = pltpu.make_async_copy(part[a].at[layer, 0], block(a, layer, chip, core), local_sem.at[j])
-        keep.start()
-        waits.append(keep.wait)
+        finish_later(pltpu.make_async_copy(part[a].at[layer, 0], block(a, layer, chip, core), local_sem.at[j, 0]), "wait")
 
     def pass_on(j):
         gather_copy(j, 0).wait_recv()
@@ -265,14 +274,14 @@
         gather_copy(j, 5).wait_recv()
         go(j, 10)
 
-    total = len(chunks)
-    start_pair(0)
-    for s in range(total + 5):
-        if s + 1 < total:
-            start_pair(s + 1)
-        for back, act in ((0, first), (1, middle), (2, final), (4, pass_on), (5, hand_over)):
-            if 0 <= s - back < total:
-                act(s - back)
+    barrier = pltpu.get_barrier_semaphore()
+    for other in (partner, right, left):
+        pl.semaphore_signal(barrier, inc=1, device_id={"dp": other}, device_id_type=MESH)
+    pl.semaphore_wait(barrier, 3)
+
+    acts = {"pair": start_pair, "first": first, "middle": middle, "final": final, "pass": pass_on, "hand": hand_over}
+    for act, j in plan:
+        acts[act](j)
 
     for q in range(shapes):
         for i in range(max(0, len(units[q]) - SETS), len(units[q])):
@@ -282,9 +291,71 @@
         wait()
 
 
+def moved(arrays, steps):
+    def body(*refs):
+        for src, dst in zip(refs[: len(arrays)], refs[len(arrays) :], strict=True):
+            dst[...] = src[...]
+
+    specs = [pl.BlockSpec((x.shape[0] // steps[0], x.shape[1] // steps[1], x.shape[2]), lambda i, j: (i, j, 0)) for x in arrays]
+    size = sum(x.size * x.dtype.itemsize for x in arrays)
+    return pl.pallas_call(
+        body,
+        out_shape=[jax.ShapeDtypeStruct(x.shape, x.dtype) for x in arrays],
+        grid=steps,
+        in_specs=specs,
+        out_specs=specs,
+        compiler_params=pltpu.CompilerParams(vmem_limit_bytes=VMEM),
+        cost_estimate=pl.CostEstimate(flops=0, bytes_accessed=2 * size, transcendentals=0),
+    )(*arrays)
+
+
+def placed(shape, chips, into, pieces):
+    arrays = [p[0] for p in pieces]
+    count = len(arrays)
+
+    def body(*refs):
+        refs = refs[0 if into is None else 1 :]
+        srcs, dst, bufs, sems = refs[:count], refs[count], refs[count + 1 : -1], refs[-1]
+        me = lax.axis_index("dp")
+        chip, core = me // CORES, me % CORES
+        rows = shape[1] // (chips * CORES)
+        ins, outs = [], []
+        for n, (x, d, other, first) in enumerate(pieces):
+            base = (lax.rem(chip + d, chips) * CORES + (1 - core if other else core)) * rows + first
+            there = dst.at[:, pl.ds(pl.multiple_of(base, STRIP), x.shape[1])]
+            ins.append(pltpu.make_async_copy(srcs[n], bufs[n], sems.at[n, 0]))
+            outs.append(pltpu.make_async_copy(bufs[n], there, sems.at[n, 1]))
+        for copy in ins:
+            copy.start()
+        for come, go in zip(ins, outs, strict=True):
+            come.wait()
+            go.start()
+        for copy in outs:
+            copy.wait()
+
+    any_space = pl.BlockSpec(memory_space=pl.ANY)
+    size = sum(x.size * x.dtype.itemsize for x in arrays)
+    return pl.pallas_call(
+        body,
+        out_shape=jax.ShapeDtypeStruct(shape, arrays[0].dtype),
+        in_specs=[any_space] * (count + (into is not None)),
+        out_specs=any_space,
+        scratch_shapes=[pltpu.VMEM(x.shape, x.dtype) for x in arrays] + [pltpu.SemaphoreType.DMA((count, 2))],
+        input_output_aliases={} if into is None else {0: 0},
+        compiler_params=pltpu.CompilerParams(vmem_limit_bytes=VMEM),
+        cost_estimate=pl.CostEstimate(flops=0, bytes_accessed=2 * size, transcendentals=0),
+    )(*(() if into is None else (into,)), *arrays)
+
+
 def solution(mesh):
     devices = mesh.shape["dp"]
     chips = devices // CORES
+
+    def hop(x, d):
+        return lax.ppermute(x, "dp", [(i, (i + d * CORES) % devices) for i in range(devices)])
+
+    def across(x):
+        return lax.ppermute(x, "dp", [(i, i // CORES * CORES + 1 - i % CORES) for i in range(devices)])
 
     def step(*arrays):
         terms, weights, m, v = (arrays[i : i + 3] for i in (0, 3, 6, 9))
@@ -296,25 +367,50 @@
         any_space = pl.BlockSpec(memory_space=pl.ANY)
         bf16 = jnp.bfloat16
         halves = [(b[0] // 2, b[1]) for b in distinct]
+        cut_rows = blocks[-1][0] // 2
         dma = pltpu.SemaphoreType.DMA
+        tail = [jax.ShapeDtypeStruct((layers, cut_rows, blocks[-1][1]), bf16)] * 2 + [jax.ShapeDtypeStruct((layers, *blocks[-1]), bf16)]
         out = pl.pallas_call(
             functools.partial(kernel, chips, layers, kinds),
-            out_shape=[jax.ShapeDtypeStruct(one.shape, one.dtype) for one in (*weights, *m, *v)],
+            out_shape=[jax.ShapeDtypeStruct(one.shape, one.dtype) for one in weights[:-1]]
+            + tail
+            + [jax.ShapeDtypeStruct(one.shape, one.dtype) for one in (*m, *v)],
             in_specs=[any_space] * 4 * count,
-            out_specs=[any_space] * 3 * count,
+            out_specs=[any_space] * (3 * count + 2),
             scratch_shapes=[pltpu.VMEM((layers, chips, *b), bf16) for b in blocks]
             + [pltpu.VMEM((layers, 6, b[0] // 2, b[1]), bf16) for b in blocks]
             + [pltpu.VMEM((SLOTS, *b), bf16) for b in halves]
             + [pltpu.VMEM((SETS, *b), jnp.float32) for b in halves] * 2
             + [pltpu.VMEM((SETS, *b), bf16) for b in halves]
             + [dma((len(distinct), SLOTS)), dma((len(distinct), SETS, 3)), dma((len(distinct), SETS, 2))]
-            + [dma((chunks * chips,))] * 2
+            + [dma((chunks * 2 * chips,))] * 2
             + [dma((chunks * 6,))] * 2
             + [dma((chunks, 11))] * 2
-            + [dma((chunks,))],
-            compiler_params=pltpu.CompilerParams(collective_id=0, has_side_effects=True, vmem_limit_bytes=62 * 1024 * 1024),
+            + [dma((chunks, 2))],
+            compiler_params=pltpu.CompilerParams(collective_id=0, has_side_effects=True, vmem_limit_bytes=VMEM),
         )(*terms, *weights, *m, *v)
-        return tuple(out)
+        new, (own_a, own_b, pair), moments = out[: count - 1], out[count - 1 : count + 2], out[count + 2 :]
+        shape, far, hold = weights[-1].shape, chips // 2, lax.optimization_barrier
+        put = functools.partial(placed, shape, chips)
+        left_a, right_b = hop(own_a, 1), hop(own_b, -1)
+        left_b, right_a = hop(own_b, 1), hop(own_a, -1)
+        results = moved([*new, *moments], (layers, chips))
+        left_a, right_b, own_a, *results = hold((left_a, right_b, own_a, *results))
+        far_a = hop(left_a, 1)
+        far_b = hop(right_b, -1)
+        over_left_a, over_right_b = across(left_a), across(right_b)
+        whole = put(None, [(own_a, 0, 0, 0), (own_b, 0, 0, cut_rows), (pair, 0, 1, 0), (left_a, chips - 1, 0, 0), (right_b, 1, 0, cut_rows)])
+        left_b, right_a, over_left_a, whole = hold((left_b, right_a, over_left_a, whole))
+        over_left_b, over_right_a = across(left_b), across(right_a)
+        whole = put(whole, [(left_b, chips - 1, 0, cut_rows), (right_a, 1, 0, 0), (over_left_a, chips - 1, 1, 0), (over_right_b, 1, 1, cut_rows)])
+        over_left_b, over_right_a, whole = hold((over_left_b, over_right_a, whole))
+        whole = put(whole, [(over_left_b, chips - 1, 1, cut_rows), (over_right_a, 1, 1, 0)])
+        far_a, far_b, whole = hold((far_a, far_b, whole))
+        over_far_a, over_far_b = across(far_a), across(far_b)
+        whole = put(whole, [(far_a, far, 0, 0), (far_b, far, 0, cut_rows)])
+        over_far_a, over_far_b, whole = hold((over_far_a, over_far_b, whole))
+        whole = put(whole, [(over_far_a, far, 1, 0), (over_far_b, far, 1, cut_rows)])
+        return (*results[: count - 1], whole, *results[count - 1 :])
 
     all_of, cut = P(None, None, None), P(None, "dp", None)
     return jax.shard_map(

time: 388 us -> 359 us (0.925)
  local copies, waits for them, and re-layouts: 45.5 us -> 0 us
  waiting for transfers between devices: 0 us -> 14.8 us
  starting transfers between devices: 0 us -> 10.6 us
  Pallas kernels: 342 us -> 332 us
    pallas_call x1, Pallas kernels: 342 us -> 288 us  [step(): pl.pallas_call(functools.partial(kernel, chips, layers, kinds), out_shape...]
    unnamed x31 -> x0, local copies, waits for them, and re-layouts: 45.5 us -> none
    pallas_call x0 -> x6, Pallas kernels: none -> 44.7 us  [the longest x1 30.3 us: moved(): pl.pallas_call(body, out_shape=[jax.ShapeDtypeStruct(x.shape, x.dtype) fo...]
    ppermute x0 -> x12, waiting for transfers between devices: none -> 14.8 us  [the longest x6 13.6 us: hop(): lax.ppermute(x, 'dp', [(i, (i + d * CORES) % devices) for i in range(devi...]
    ppermute x0 -> x12, starting transfers between devices: none -> 10.6 us  [the longest x6 6.99 us: hop(): lax.ppermute(x, 'dp', [(i, (i + d * CORES) % devices) for i in range(devi...]
  transfers between devices with their start and end apart: 0 -> 12, of which waited for: 0 -> 2; matrix products, arithmetic and copies ran while one was open for 0% -> 0% of each run, Pallas kernels for 0% -> 12%
where the time goes in v2:
time: 359 us; the launch traced here: 358 us
  Pallas kernels  332 us (92%)
  waiting for transfers between devices  14.8 us (4%)
  starting transfers between devices  10.6 us (3%)
    pallas_call x1, Pallas kernels, step(): pl.pallas_call(functools.partial(kernel, chips, layers, kinds), out_shape...  288 us
    pallas_call x1, Pallas kernels, moved(): pl.pallas_call(body, out_shape=[jax.ShapeDtypeStruct(x.shape, x.dtype) fo...  30.3 us
    pallas_call x5, Pallas kernels, placed(): pl.pallas_call(body, out_shape=jax.ShapeDtypeStruct(shape, arrays[0].dtyp...  14.4 us
    ppermute x6, waiting for transfers between devices, hop(): lax.ppermute(x, 'dp', [(i, (i + d * CORES) % devices) for i in range(devi...  13.6 us
  transfers between devices with their start and end apart: 12, of which 2 were waited for; matrix products, arithmetic and copies ran while one was open for 0% of the time, Pallas kernels for 12%

profile of v2, /device:TPU:113, one launch (start us, length us, event | category | flops | bytes accessed | tf_op | source)
XLA Modules:
  0.0 358.5 jit_solution(3614785355315702265)
XLA Ops:
  0.6 287.7 %shard_map.187 = (bf16[2,1024,3328]{2,1,0:T(8,128)(2,1)}, bf16[2,1024,3328]{2,1,0:T(8,128)(2,1)}, bf16[2,208,1024]{2,1,0:T(8,128)(2,1)}, bf16[2,208,1024]{2,1,0:...) custom-call(bf16[1,2,1024,3328]{3,2,1,0:T(8,128)(2,1)} %refs_0_.1, ...), custom_call_target="tpu_custom_call" | custom-call | tf_op jit(solution)/shard_map/pallas_call | solution.py:373
  288.3 0.8 collective-permute-start
  289.1 2.0 collective-permute-start.1
  291.1 0.7 collective-permute-start.5
  291.8 0.8 collective-permute-start.4
  292.5 30.3 %shard_map.188 = (bf16[2,1024,3328]{2,1,0:T(8,128)(2,1)}, bf16[2,1024,3328]{2,1,0:T(8,128)(2,1)}, f32[2,128,3328]{2,1,0:T(8,128)}, f32[2,128,3328]{2,1,0:T(8,128...) custom-call(bf16[2,1024,3328]{2,1,0:T(8,128)(2,1)} %get-tuple-element., ...), custom_call_target="tpu_custom_call" | custom-call | bytes 95420416 | tf_op jit(solution)/shard_map/pallas_call | solution.py:301
  322.9 0.0 collective-permute-done.refs_3_
  322.9 0.0 collective-permute-done.1.refs_4_
  322.9 1.3 collective-permute-start.6
  324.2 0.1 collective-permute-start.9
  324.3 4.3 %shard_map.189.refs_0_ = bf16[2,3328,1024]{2,1,0:T(8,128)(2,1)} custom-call(bf16[2,208,1024]{2,1,0:T(8,128)(2,1)} %get-tuple-element.74.refs_0_, bf16[2,208,1024]{2,1,0:T(8,128)(2,1)} %get-tuple-element.53.refs_1_, bf16[2,416,1024]{2,1,0:T(8,128)(2,1)} %get-tuple-element.75.refs_2_, bf16[2,208,1024]{2,1,0:T(8,128)(2,1)} %collective-permute-done.refs_3_, ...), custom_call_target="tpu_custom_call" | custom-call | bytes 10223616 | tf_op jit(solution)/shard_map/pallas_call | solution.py:338
  328.6 0.0 collective-permute-done.5.refs_2_
  328.6 0.0 collective-permute-done.4.refs_1_
  328.7 0.0 collective-permute-done.6.refs_3_
  328.7 0.9 collective-permute-start.7
  329.5 0.0 collective-permute-start.8
  329.5 0.2 collective-permute-start.2
  329.7 2.6 collective-permute-start.3
  332.3 0.0 collective-permute-done.9.refs_4_
  332.3 3.0 shard_map.190.refs_0_
  335.3 0.0 collective-permute-done.7.refs_1_
  335.3 0.0 collective-permute-done.8.refs_2_
  335.3 2.4 shard_map.191.refs_0_
  337.7 13.6 %collective-permute-done.2.refs_1_ = bf16[2,208,1024]{2,1,0:T(8,128)(2,1)} collective-permute-done((bf16[2,208,1024]{2,1,0:T(8,128)(2,1)}, bf16[2,208,1024]{2,1,0:T(8,128)(2,1)}, u32[]{:S(2)}, u32[]{:S(2)}) %collective-permute-start.2) | collective-permute-done | bytes 852000 | tf_op jit(solution)/shard_map/ppermute | solution.py:355
  351.3 0.0 collective-permute-done.3.refs_2_
  351.3 1.3 collective-permute-start.10
  352.5 0.0 collective-permute-start.11
  352.5 2.4 shard_map.192.refs_0_
  354.9 0.0 collective-permute-done.10.refs_1_
  354.9 1.2 collective-permute-done.11.refs_2_
  356.1 2.4 shard_map.193
Async XLA Ops:
  288.3 34.5 %collective-permute-start = (bf16[2,208,1024]{2,1,0:T(8,128)(2,1)}, bf16[2,208,1024]{2,1,0:T(8,128)(2,1)}, u32[]{:S(2)}, u32[]{:S(2)}) collective-permute-start(bf16[2,208,1024]{2,1,0:T(8,128)(2,1)} %get-tuple-element.74.refs_0_), channel_id=1, source_target_pairs={{0,2},{1,3},{2,4},{3,5},{4,6},{5,7},{6,0},{7,1},{8,10},{9,11},{10,... | collective-permute-start | bytes 2555912 | tf_op jit(solution)/shard_map/ppermute | solution.py:355
  289.1 33.8 %collective-permute-start.1 = (bf16[2,208,1024]{2,1,0:T(8,128)(2,1)}, bf16[2,208,1024]{2,1,0:T(8,128)(2,1)}, u32[]{:S(2)}, u32[]{:S(2)}) collective-permute-start(bf16[2,208,1024]{2,1,0:T(8,128)(2,1)} %get-tuple-element.53.refs_1_), channel_id=1, source_target_pairs={{0,6},{1,7},{2,0},{3,1},{4,2},{5,3},{6,4},{7,5},{8,14},{9,15},{10,... | collective-permute-start | bytes 2555912 | tf_op jit(solution)/shard_map/ppermute | solution.py:355
  291.1 37.6 %collective-permute-start.5 = (bf16[2,208,1024]{2,1,0:T(8,128)(2,1)}, bf16[2,208,1024]{2,1,0:T(8,128)(2,1)}, u32[]{:S(2)}, u32[]{:S(2)}) collective-permute-start(bf16[2,208,1024]{2,1,0:T(8,128)(2,1)} %get-tuple-element.74.refs_0_), channel_id=1, source_target_pairs={{0,6},{1,7},{2,0},{3,1},{4,2},{5,3},{6,4},{7,5},{8,14},{9,15},{10,... | collective-permute-start | bytes 2555912 | tf_op jit(solution)/shard_map/ppermute | solution.py:355
  291.8 36.9 %collective-permute-start.4 = (bf16[2,208,1024]{2,1,0:T(8,128)(2,1)}, bf16[2,208,1024]{2,1,0:T(8,128)(2,1)}, u32[]{:S(2)}, u32[]{:S(2)}) collective-permute-start(bf16[2,208,1024]{2,1,0:T(8,128)(2,1)} %get-tuple-element.53.refs_1_), channel_id=1, source_target_pairs={{0,2},{1,3},{2,4},{3,5},{4,6},{5,7},{6,0},{7,1},{8,10},{9,11},{10,... | collective-permute-start | bytes 2555912 | tf_op jit(solution)/shard_map/ppermute | solution.py:355
  322.9 5.8 %collective-permute-start.6 = (bf16[2,208,1024]{2,1,0:T(8,128)(2,1)}, bf16[2,208,1024]{2,1,0:T(8,128)(2,1)}, u32[]{:S(2)}, u32[]{:S(2)}) collective-permute-start(bf16[2,208,1024]{2,1,0:T(8,128)(2,1)} %collective-permute-done.refs_3_), channel_id=1, source_target_pairs={{0,1},{1,0},{2,3},{3,2},{4,5},{5,4},{6,7},{7,6},{8,9},{9,8},{10,11... | collective-permute-start | bytes 2555912 | tf_op jit(solution)/shard_map/ppermute | solution.py:358
  324.2 8.1 %collective-permute-start.9 = (bf16[2,208,1024]{2,1,0:T(8,128)(2,1)}, bf16[2,208,1024]{2,1,0:T(8,128)(2,1)}, u32[]{:S(2)}, u32[]{:S(2)}) collective-permute-start(bf16[2,208,1024]{2,1,0:T(8,128)(2,1)} %collective-permute-done.1.refs_4_), channel_id=1, source_target_pairs={{0,1},{1,0},{2,3},{3,2},{4,5},{5,4},{6,7},{7,6},{8,9},{9,8},{10,11... | collective-permute-start | bytes 2555912 | tf_op jit(solution)/shard_map/ppermute | solution.py:358
  328.7 6.6 %collective-permute-start.7 = (bf16[2,208,1024]{2,1,0:T(8,128)(2,1)}, bf16[2,208,1024]{2,1,0:T(8,128)(2,1)}, u32[]{:S(2)}, u32[]{:S(2)}) collective-permute-start(bf16[2,208,1024]{2,1,0:T(8,128)(2,1)} %collective-permute-done.4.refs_1_), channel_id=1, source_target_pairs={{0,1},{1,0},{2,3},{3,2},{4,5},{5,4},{6,7},{7,6},{8,9},{9,8},{10,11... | collective-permute-start | bytes 2555912 | tf_op jit(solution)/shard_map/ppermute | solution.py:358
  329.5 5.8 %collective-permute-start.8 = (bf16[2,208,1024]{2,1,0:T(8,128)(2,1)}, bf16[2,208,1024]{2,1,0:T(8,128)(2,1)}, u32[]{:S(2)}, u32[]{:S(2)}) collective-permute-start(bf16[2,208,1024]{2,1,0:T(8,128)(2,1)} %collective-permute-done.5.refs_2_), channel_id=1, source_target_pairs={{0,1},{1,0},{2,3},{3,2},{4,5},{5,4},{6,7},{7,6},{8,9},{9,8},{10,11... | collective-permute-start | bytes 2555912 | tf_op jit(solution)/shard_map/ppermute | solution.py:358
  329.5 21.7 %collective-permute-start.2 = (bf16[2,208,1024]{2,1,0:T(8,128)(2,1)}, bf16[2,208,1024]{2,1,0:T(8,128)(2,1)}, u32[]{:S(2)}, u32[]{:S(2)}) collective-permute-start(bf16[2,208,1024]{2,1,0:T(8,128)(2,1)} %collective-permute-done.refs_3_), channel_id=1, source_target_pairs={{0,2},{1,3},{2,4},{3,5},{4,6},{5,7},{6,0},{7,1},{8,10},{9,11},{10,... | collective-permute-start | bytes 2555912 | tf_op jit(solution)/shard_map/ppermute | solution.py:355
  329.7 21.5 %collective-permute-start.3 = (bf16[2,208,1024]{2,1,0:T(8,128)(2,1)}, bf16[2,208,1024]{2,1,0:T(8,128)(2,1)}, u32[]{:S(2)}, u32[]{:S(2)}) collective-permute-start(bf16[2,208,1024]{2,1,0:T(8,128)(2,1)} %collective-permute-done.1.refs_4_), channel_id=1, source_target_pairs={{0,6},{1,7},{2,0},{3,1},{4,2},{5,3},{6,4},{7,5},{8,14},{9,15},{10,... | collective-permute-start | bytes 2555912 | tf_op jit(solution)/shard_map/ppermute | solution.py:355
  351.3 3.7 %collective-permute-start.10 = (bf16[2,208,1024]{2,1,0:T(8,128)(2,1)}, bf16[2,208,1024]{2,1,0:T(8,128)(2,1)}, u32[]{:S(2)}, u32[]{:S(2)}) collective-permute-start(bf16[2,208,1024]{2,1,0:T(8,128)(2,1)} %collective-permute-done.2.refs_1_), channel_id=1, source_target_pairs={{0,1},{1,0},{2,3},{3,2},{4,5},{5,4},{6,7},{7,6},{8,9},{9,8},{10,11... | collective-permute-start | bytes 2555912 | tf_op jit(solution)/shard_map/ppermute | solution.py:358
  352.5 3.6 collective-permute-start.11

commit v3 on v2

--- a/solution.py
+++ b/solution.py
@@ -1,4 +1,5 @@
 import functools
+import itertools
 
 import jax
 import jax.numpy as jnp
@@ -13,6 +14,7 @@
 STRIP = 16
 SLOTS = 6
 VMEM = 67043328
+LEAD = 0
 SETS = 3
 
 
@@ -34,12 +36,11 @@
     take = iter(refs)
     g, w, m, v = ([next(take) for _ in range(count)] for _ in range(4))
     w_out = [next(take) for _ in range(last)]
-    new_half = [next(take) for _ in range(2)]
-    new_pair = next(take)
+    new_half, new_pair, far_half = [next(take) for _ in range(2)], next(take), [next(take) for _ in range(2)]
     m_out, v_out, part, arrived = ([next(take) for _ in range(count)] for _ in range(4))
     shapes = max(kinds) + 1
     own, m_set, v_set, w_set = ([next(take) for _ in range(shapes)] for _ in range(4))
-    own_sem, set_in, set_out, pair_send, pair_recv, ring_send, ring_recv, gather_send, gather_recv, local_sem = take
+    own_sem, set_in, set_out, pair_send, pair_recv, ring_send, ring_recv, gather_send, gather_recv, local_sem, early_pair_send, early_pair_recv, early_ring_send, early_ring_recv, turn_sem = take
 
     me = lax.axis_index("dp")
     chip, core = me // CORES, me % CORES
@@ -63,22 +64,33 @@
 
     order = ((far, 0), (far, 1), (1, 1), (chips - 1, 0), (1, 0), (chips - 1, 1), (0, 0), (0, 1))
 
-    def pair_copy(j, d, h):
-        a, layer = chunks[j]
-        src = g[a].at[0, layer, pl.ds(pl.multiple_of((turn[d] * CORES + 1 - core) * rows[a] + h * half[a], STRIP), half[a])]
+    def pieces(j, d, h):
+        size = half[chunks[j][0]]
+        if j == 0 and d == far:
+            return [(n, h * size + n * STRIP, STRIP) for n in range(size // STRIP)]
+        return [(None, h * size, size)]
+
+    def pair_copy(j, d, h, piece):
+        a, layer = chunks[j]
+        n, row, size = piece
+        src = g[a].at[0, layer, pl.ds(pl.multiple_of((turn[d] * CORES + 1 - core) * rows[a] + row, STRIP), size)]
         s = j * len(order) + order.index((d, h))
-        return remote(src, part[a].at[layer, d, pl.ds(h * half[a], half[a])], pair_send.at[s], pair_recv.at[s], partner)
+        sems = (pair_send.at[s], pair_recv.at[s]) if n is None else (early_pair_send.at[h, n], early_pair_recv.at[h, n])
+        return remote(src, part[a].at[layer, d, pl.ds(row, size)], *sems, partner)
 
     def start_pair(j):
-        for d, h in order:
-            finish_later(pair_copy(j, d, h), "wait_send")
+        copies = [[(d, h, piece) for piece in pieces(j, d, h)] for d, h in order]
+        for together in [*zip(*copies[:2], strict=True), *copies[2:]]:
+            for one in together:
+                finish_later(pair_copy(j, *one), "wait_send")
 
     total = len(chunks)
     gathered = [j for j in range(total) if chunks[j][0] != last]
-    plan = [("pair", 0)]
+    plan = [("pair", 0), ("follow", 0)]
     for s in range(total):
         plan += [("first", s)]
         plan += [("pair", s + 1)] if s + 1 < total else []
+        plan += [("lead", s)] if s == 0 else []
         plan += [("middle", s - 1)] if s >= 1 else []
         plan += [("middle", s)] if s == total - 1 else []
         plan += [("final", s - 2)] if s >= 2 else []
@@ -113,7 +125,6 @@
         i = used[q]
         used[q] += 1
         assert of_kind[q][i] == (j, d, h)
-        pair_copy(j, d, h).wait_recv()
         own_copy(q, i).wait()
         mine = own[q].at[i % SLOTS]
         total = part[a].at[layer, d, pl.ds(h * half[a], half[a])]
@@ -125,41 +136,75 @@
             x = x.astype(jnp.bfloat16)
             total[strip, :] = x if finish is None else finish(strip, f32(x))
 
-        strips(half[a], body)
+        for piece in pieces(j, d, h):
+            pair_copy(j, d, h, piece).wait_recv()
+            if piece[0] is None:
+                strips(half[a], body)
+            else:
+                body(pl.ds(piece[1] - h * half[a], piece[2]))
+                yield piece
         if i + SLOTS < len(of_kind[q]):
             own_copy(q, i + SLOTS).start()
-        return total
-
-    def ring_copy(j, slot):
-        a, layer = chunks[j]
-        d, h = ((far, 0), (1, 1), (1, 0), (far, 1), (chips - 1, 0), (chips - 1, 1))[slot]
-        src = part[a].at[layer, d, pl.ds(h * half[a], half[a])]
+
+    def do(work):
+        for _ in work:
+            pass
+
+    ring_slots = ((far, 0), (1, 1), (1, 0), (far, 1), (chips - 1, 0), (chips - 1, 1))
+
+    def ring_copy(j, slot, piece):
+        a, layer = chunks[j]
+        n, row, size = piece
+        d, h = ring_slots[slot]
+        src = part[a].at[layer, d, pl.ds(row, size)]
+        dst = arrived[a].at[layer, slot, pl.ds(row - h * half[a], size)]
         s = j * 6 + slot
-        return remote(src, arrived[a].at[layer, slot], ring_send.at[s], ring_recv.at[s], right if slot < 3 else left)
+        sems = (ring_send.at[s], ring_recv.at[s]) if n is None else (early_ring_send.at[h, n], early_ring_recv.at[h, n])
+        return remote(src, dst, *sems, right if slot < 3 else left)
 
     def send(j, slot):
-        finish_later(ring_copy(j, slot), "wait_send")
+        for piece in pieces(j, *ring_slots[slot]):
+            finish_later(ring_copy(j, slot, piece), "wait_send")
+
+    come = set()
 
     def arrival(j, slot):
-        ring_copy(j, slot).wait_recv()
+        for piece in [] if (j, slot) in come else pieces(j, *ring_slots[slot]):
+            ring_copy(j, slot, piece).wait_recv()
+        come.add((j, slot))
         a, layer = chunks[j]
         return arrived[a].at[layer, slot]
 
+    def follow(j):
+        @pl.when(core == 1)
+        def _():
+            pl.semaphore_wait(turn_sem, 1)
+
+    def lead(j):
+        arrival(j, LEAD)
+
+        @pl.when(core == 0)
+        def _():
+            pl.semaphore_signal(turn_sem, inc=1, device_id={"dp": partner}, device_id_type=MESH)
+
+    def add_and_send(j, slot, extra=()):
+        do(add_own(j, *ring_slots[slot], extra))
+        send(j, slot)
+
     def first(j):
-        add_own(j, far, 0, ())
-        send(j, 0)
-        add_own(j, far, 1, ())
-        send(j, 3)
-        add_own(j, 1, 1, ())
-        send(j, 1)
-        add_own(j, chips - 1, 0, ())
-        send(j, 4)
+        if pieces(j, far, 0)[0][0] is None:
+            add_and_send(j, 0)
+            add_and_send(j, 3)
+        else:
+            for both in itertools.zip_longest(add_own(j, far, 0, ()), add_own(j, far, 1, ())):
+                for slot, piece in zip((0, 3), both, strict=True):
+                    finish_later(ring_copy(j, slot, piece), "wait_send")
+        add_and_send(j, 1)
+        add_and_send(j, 4)
 
     def middle(j):
-        add_own(j, 1, 0, (arrival(j, 0),))
-        send(j, 2)
-        add_own(j, chips - 1, 1, (arrival(j, 3),))
-        send(j, 5)
+        add_and_send(j, 2, (arrival(j, 0),))
+        add_and_send(j, 5, (arrival(j, 3),))
 
     units = [[(j, h) for j in range(len(chunks)) for h in range(2) if kinds[chunks[j][0]] == q] for q in range(shapes)]
 
@@ -208,7 +253,7 @@
             step = new_m * lax.rsqrt(new_v + 1e-8) + 0.1 * old
             return (old - 0.02 * step).astype(jnp.bfloat16)
 
-        add_own(j, 0, h, extra, finish)
+        do(add_own(j, 0, h, extra, finish))
         for copy in outs:
             copy.start()
         start_set(q, i + SETS - 1)
@@ -229,7 +274,7 @@
         if n < 6:
             d, h, to = ((chips - 1, 0, right), (1, 1, left))[n - 4]
             there = block(a, layer, turn[d], core, h)
-            return remote(there, there, *s, to)
+            return remote(there, far_half[h].at[layer] if a == last - 1 else there, *s, to)
         if n == 6:
             return remote(part[a].at[layer, 0], block(a, layer, chip, core), *s, partner)
         d, h = ((chips - 1, None), (1, None), (far, 0), (far, 1))[n - 7]
@@ -269,17 +314,17 @@
         go(j, 8)
 
     def hand_over(j):
-        gather_copy(j, 4).wait_recv()
-        go(j, 9)
-        gather_copy(j, 5).wait_recv()
-        go(j, 10)
+        for n, then in ((4, 9), (5, 10)):
+            gather_copy(j, n).wait_recv()
+            if chunks[j][0] != last - 1:
+                go(j, then)
 
     barrier = pltpu.get_barrier_semaphore()
     for other in (partner, right, left):
         pl.semaphore_signal(barrier, inc=1, device_id={"dp": other}, device_id_type=MESH)
     pl.semaphore_wait(barrier, 3)
 
-    acts = {"pair": start_pair, "first": first, "middle": middle, "final": final, "pass": pass_on, "hand": hand_over}
+    acts = {"pair": start_pair, "follow": follow, "lead": lead, "first": first, "middle": middle, "final": final, "pass": pass_on, "hand": hand_over}
     for act, j in plan:
         acts[act](j)
 
@@ -369,14 +414,16 @@
         halves = [(b[0] // 2, b[1]) for b in distinct]
         cut_rows = blocks[-1][0] // 2
         dma = pltpu.SemaphoreType.DMA
-        tail = [jax.ShapeDtypeStruct((layers, cut_rows, blocks[-1][1]), bf16)] * 2 + [jax.ShapeDtypeStruct((layers, *blocks[-1]), bf16)]
+        cut_cols, (far_rows, far_cols) = blocks[-1][1], (blocks[-2][0] // 2, blocks[-2][1])
+        tail = [(layers, cut_rows, cut_cols)] * 2 + [(layers, *blocks[-1])] + [(layers, far_rows, far_cols)] * 2
+        early = (2, blocks[0][0] // 2 // STRIP)
         out = pl.pallas_call(
             functools.partial(kernel, chips, layers, kinds),
             out_shape=[jax.ShapeDtypeStruct(one.shape, one.dtype) for one in weights[:-1]]
-            + tail
+            + [jax.ShapeDtypeStruct(one, bf16) for one in tail]
             + [jax.ShapeDtypeStruct(one.shape, one.dtype) for one in (*m, *v)],
             in_specs=[any_space] * 4 * count,
-            out_specs=[any_space] * (3 * count + 2),
+            out_specs=[any_space] * (3 * count - 1 + len(tail)),
             scratch_shapes=[pltpu.VMEM((layers, chips, *b), bf16) for b in blocks]
             + [pltpu.VMEM((layers, 6, b[0] // 2, b[1]), bf16) for b in blocks]
             + [pltpu.VMEM((SLOTS, *b), bf16) for b in halves]
@@ -386,26 +433,31 @@
             + [dma((chunks * 2 * chips,))] * 2
             + [dma((chunks * 6,))] * 2
             + [dma((chunks, 11))] * 2
-            + [dma((chunks, 2))],
+            + [dma((chunks, 2))]
+            + [dma(early)] * 4
+            + [pltpu.SemaphoreType.REGULAR],
             compiler_params=pltpu.CompilerParams(collective_id=0, has_side_effects=True, vmem_limit_bytes=VMEM),
         )(*terms, *weights, *m, *v)
-        new, (own_a, own_b, pair), moments = out[: count - 1], out[count - 1 : count + 2], out[count + 2 :]
+        new, (own_a, own_b, pair, late_a, late_b), moments = out[: count - 1], out[count - 1 : count - 1 + len(tail)], out[count - 1 + len(tail) :]
         shape, far, hold = weights[-1].shape, chips // 2, lax.optimization_barrier
         put = functools.partial(placed, shape, chips)
         left_a, right_b = hop(own_a, 1), hop(own_b, -1)
         left_b, right_a = hop(own_b, 1), hop(own_a, -1)
-        results = moved([*new, *moments], (layers, chips))
-        left_a, right_b, own_a, *results = hold((left_a, right_b, own_a, *results))
-        far_a = hop(left_a, 1)
-        far_b = hop(right_b, -1)
-        over_left_a, over_right_b = across(left_a), across(right_b)
-        whole = put(None, [(own_a, 0, 0, 0), (own_b, 0, 0, cut_rows), (pair, 0, 1, 0), (left_a, chips - 1, 0, 0), (right_b, 1, 0, cut_rows)])
-        left_b, right_a, over_left_a, whole = hold((left_b, right_a, over_left_a, whole))
-        over_left_b, over_right_a = across(left_b), across(right_a)
-        whole = put(whole, [(left_b, chips - 1, 0, cut_rows), (right_a, 1, 0, 0), (over_left_a, chips - 1, 1, 0), (over_right_b, 1, 1, cut_rows)])
-        over_left_b, over_right_a, whole = hold((over_left_b, over_right_a, whole))
-        whole = put(whole, [(over_left_b, chips - 1, 1, cut_rows), (over_right_a, 1, 1, 0)])
-        far_a, far_b, whole = hold((far_a, far_b, whole))
+        results = list(moved([*new, *moments], (layers, chips)))
+        left_a, right_b, own_a, results = hold((left_a, right_b, own_a, results))
+        far_a, far_b = hop(left_a, 1), hop(right_b, -1)
+        start = [(own_a, 0, 0, 0), (own_b, 0, 0, cut_rows), (pair, 0, 1, 0), (left_a, chips - 1, 0, 0), (right_b, 1, 0, cut_rows)]
+        whole = put(None, start)
+        left_a, right_b, left_b, right_a, late_a, late_b, whole = hold((left_a, right_b, left_b, right_a, late_a, late_b, whole))
+        over = [across(x) for x in (left_a, right_b, left_b, right_a)]
+        over_late = across(late_a), across(late_b)
+        whole = put(whole, [(left_b, chips - 1, 0, cut_rows), (right_a, 1, 0, 0)])
+        over, whole = hold((over, whole))
+        whole = put(whole, [(x, d, 1, row) for x, d, row in zip(over, (chips - 1, 1, chips - 1, 1), (0, cut_rows, cut_rows, 0), strict=True)])
+        over_late, whole, results = hold((over_late, whole, results))
+        late = [(x, far, other, row) for other, two in enumerate(((late_a, late_b), over_late)) for x, row in zip(two, (0, far_rows), strict=True)]
+        results[count - 2] = placed(weights[-2].shape, chips, results[count - 2], late)
+        far_a, far_b, whole, results = hold((far_a, far_b, whole, results))
         over_far_a, over_far_b = across(far_a), across(far_b)
         whole = put(whole, [(far_a, far, 0, 0), (far_b, far, 0, cut_rows)])
         over_far_a, over_far_b, whole = hold((over_far_a, over_far_b, whole))

time: 359 us -> 358 us (level)
    ppermute x6 -> x8, waiting for transfers between devices: 1.19 us -> 5.08 us  [across(): lax.ppermute(x, 'dp', [(i, i // CORES * CORES + 1 - i % CORES) for i in r...]
    pallas_call x5 -> x6, Pallas kernels: 14.4 us -> 17.4 us  [placed(): pl.pallas_call(body, out_shape=jax.ShapeDtypeStruct(shape, arrays[0].dtyp...]
  transfers between devices with their start and end apart: 12 -> 14, of which waited for: 2 -> 5; matrix products, arithmetic and copies ran while one was open for 0% -> 0% of each run, Pallas kernels for 12% -> 13%
where the time goes in v3:
time: 358 us; the launch traced here: 357 us
  Pallas kernels  333 us (93%)
  waiting for transfers between devices  15.3 us (4%)
  starting transfers between devices  8.65 us (2%)
    pallas_call x1, Pallas kernels, step(): pl.pallas_call(functools.partial(kernel, chips, layers, kinds), out_shape...  285 us
    pallas_call x1, Pallas kernels, moved(): pl.pallas_call(body, out_shape=[jax.ShapeDtypeStruct(x.shape, x.dtype) fo...  30.3 us
    pallas_call x6, Pallas kernels, placed(): pl.pallas_call(body, out_shape=jax.ShapeDtypeStruct(shape, arrays[0].dtyp...  17.4 us
    ppermute x6, waiting for transfers between devices, hop(): lax.ppermute(x, 'dp', [(i, (i + d * CORES) % devices) for i in range(devi...  10.2 us
  transfers between devices with their start and end apart: 14, of which 5 were waited for; matrix products, arithmetic and copies ran while one was open for 0% of the time, Pallas kernels for 13%

profile of v3, /device:TPU:113, one launch (start us, length us, event | category | flops | bytes accessed | tf_op | source)
XLA Modules:
  0.0 357.4 jit_solution(10441996994785751179)
XLA Ops:
  0.6 285.0 %shard_map.187 = (bf16[2,1024,3328]{2,1,0:T(8,128)(2,1)}, bf16[2,1024,3328]{2,1,0:T(8,128)(2,1)}, bf16[2,208,1024]{2,1,0:T(8,128)(2,1)}, bf16[2,208,1024]{2,1,0:...) custom-call(bf16[1,2,1024,3328]{3,2,1,0:T(8,128)(2,1)} %refs_0_.1, ...), custom_call_target="tpu_custom_call" | custom-call | tf_op jit(solution)/shard_map/pallas_call | solution.py:420
  285.6 1.0 collective-permute-start
  286.6 1.8 collective-permute-start.1
  288.4 0.9 collective-permute-start.5
  289.3 0.6 collective-permute-start.4
  289.8 30.3 %shard_map.188 = (bf16[2,1024,3328]{2,1,0:T(8,128)(2,1)}, bf16[2,1024,3328]{2,1,0:T(8,128)(2,1)}, f32[2,128,3328]{2,1,0:T(8,128)}, f32[2,128,3328]{2,1,0:T(8,128...) custom-call(bf16[2,1024,3328]{2,1,0:T(8,128)(2,1)} %get-tuple-element., ...), custom_call_target="tpu_custom_call" | custom-call | bytes 95420416 | tf_op jit(solution)/shard_map/pallas_call | solution.py:346
  320.2 0.0 collective-permute-done.refs_3_
  320.2 0.0 collective-permute-done.1.refs_4_
  320.2 4.3 %shard_map.189.refs_0_ = bf16[2,3328,1024]{2,1,0:T(8,128)(2,1)} custom-call(bf16[2,208,1024]{2,1,0:T(8,128)(2,1)} %get-tuple-element.100.refs_0_, bf16[2,208,1024]{2,1,0:T(8,128)(2,1)} %get-tuple-element.79.refs_1_, bf16[2,416,1024]{2,1,0:T(8,128)(2,1)} %get-tuple-element.101.refs_2_, bf16[2,208,1024]{2,1,0:T(8,128)(2,1)} %collective-permute-done.refs_3_, ...), custom_call_target="tpu_custom_call" | custom-call | bytes 10223616 | tf_op jit(solution)/shard_map/pallas_call | solution.py:383
  324.5 0.0 collective-permute-done.5.refs_2_
  324.5 0.0 collective-permute-done.4.refs_1_
  324.5 0.1 collective-permute-start.8
  324.6 0.5 collective-permute-start.9
  325.1 0.1 collective-permute-start.10
  325.2 0.4 collective-permute-start.11
  325.6 0.1 collective-permute-start.6
  325.7 1.6 collective-permute-done.8.refs_1_
  327.3 0.1 collective-permute-start.7
  327.5 1.1 collective-permute-done.9.refs_2_
  328.6 0.0 collective-permute-start.2
  328.6 1.2 collective-permute-done.10.refs_3_
  329.8 2.1 collective-permute-start.3
  331.9 2.4 shard_map.190.refs_0_
  334.3 0.0 collective-permute-done.11.refs_4_
  334.3 3.0 shard_map.191.refs_0_
  337.3 0.0 collective-permute-done.6.refs_3_
  337.3 0.0 collective-permute-done.7.refs_4_
  337.3 3.0 shard_map.192
  340.3 10.2 %collective-permute-done.2.refs_1_ = bf16[2,208,1024]{2,1,0:T(8,128)(2,1)} collective-permute-done((bf16[2,208,1024]{2,1,0:T(8,128)(2,1)}, bf16[2,208,1024]{2,1,0:T(8,128)(2,1)}, u32[]{:S(2)}, u32[]{:S(2)}) %collective-permute-start.2) | collective-permute-done | bytes 852000 | tf_op jit(solution)/shard_map/ppermute | solution.py:400
  350.4 0.0 collective-permute-done.3.refs_2_
  350.5 1.0 collective-permute-start.12
  351.5 0.0 collective-permute-start.13
  351.5 2.4 shard_map.193.refs_0_
  353.8 0.0 collective-permute-done.12.refs_1_
  353.8 1.2 collective-permute-done.13.refs_2_
  355.0 2.4 shard_map.194
Async XLA Ops:
  285.6 34.5 %collective-permute-start = (bf16[2,208,1024]{2,1,0:T(8,128)(2,1)}, bf16[2,208,1024]{2,1,0:T(8,128)(2,1)}, u32[]{:S(2)}, u32[]{:S(2)}) collective-permute-start(bf16[2,208,1024]{2,1,0:T(8,128)(2,1)} %get-tuple-element.100.refs_0_), channel_id=1, source_target_pairs={{0,2},{1,3},{2,4},{3,5},{4,6},{5,7},{6,0},{7,1},{8,10},{9,11},{10,... | collective-permute-start | bytes 2555912 | tf_op jit(solution)/shard_map/ppermute | solution.py:400
  286.6 33.6 %collective-permute-start.1 = (bf16[2,208,1024]{2,1,0:T(8,128)(2,1)}, bf16[2,208,1024]{2,1,0:T(8,128)(2,1)}, u32[]{:S(2)}, u32[]{:S(2)}) collective-permute-start(bf16[2,208,1024]{2,1,0:T(8,128)(2,1)} %get-tuple-element.79.refs_1_), channel_id=1, source_target_pairs={{0,6},{1,7},{2,0},{3,1},{4,2},{5,3},{6,4},{7,5},{8,14},{9,15},{10,... | collective-permute-start | bytes 2555912 | tf_op jit(solution)/shard_map/ppermute | solution.py:400
  288.4 36.2 %collective-permute-start.5 = (bf16[2,208,1024]{2,1,0:T(8,128)(2,1)}, bf16[2,208,1024]{2,1,0:T(8,128)(2,1)}, u32[]{:S(2)}, u32[]{:S(2)}) collective-permute-start(bf16[2,208,1024]{2,1,0:T(8,128)(2,1)} %get-tuple-element.100.refs_0_), channel_id=1, source_target_pairs={{0,6},{1,7},{2,0},{3,1},{4,2},{5,3},{6,4},{7,5},{8,14},{9,15},{10,... | collective-permute-start | bytes 2555912 | tf_op jit(solution)/shard_map/ppermute | solution.py:400
  289.3 35.3 %collective-permute-start.4 = (bf16[2,208,1024]{2,1,0:T(8,128)(2,1)}, bf16[2,208,1024]{2,1,0:T(8,128)(2,1)}, u32[]{:S(2)}, u32[]{:S(2)}) collective-permute-start(bf16[2,208,1024]{2,1,0:T(8,128)(2,1)} %get-tuple-element.79.refs_1_), channel_id=1, source_target_pairs={{0,2},{1,3},{2,4},{3,5},{4,6},{5,7},{6,0},{7,1},{8,10},{9,11},{10,... | collective-permute-start | bytes 2555912 | tf_op jit(solution)/shard_map/ppermute | solution.py:400
  324.5 2.8 collective-permute-start.8
  324.6 3.9 %collective-permute-start.9 = (bf16[2,208,1024]{2,1,0:T(8,128)(2,1)}, bf16[2,208,1024]{2,1,0:T(8,128)(2,1)}, u32[]{:S(2)}, u32[]{:S(2)}) collective-permute-start(bf16[2,208,1024]{2,1,0:T(8,128)(2,1)} %collective-permute-done.1.refs_4_), channel_id=1, source_target_pairs={{0,1},{1,0},{2,3},{3,2},{4,5},{5,4},{6,7},{7,6},{8,9},{9,8},{10,11... | collective-permute-start | bytes 2555912 | tf_op jit(solution)/shard_map/ppermute | solution.py:403
  325.1 4.6 %collective-permute-start.10 = (bf16[2,208,1024]{2,1,0:T(8,128)(2,1)}, bf16[2,208,1024]{2,1,0:T(8,128)(2,1)}, u32[]{:S(2)}, u32[]{:S(2)}) collective-permute-start(bf16[2,208,1024]{2,1,0:T(8,128)(2,1)} %collective-permute-done.4.refs_1_), channel_id=1, source_target_pairs={{0,1},{1,0},{2,3},{3,2},{4,5},{5,4},{6,7},{7,6},{8,9},{9,8},{10,11... | collective-permute-start | bytes 2555912 | tf_op jit(solution)/shard_map/ppermute | solution.py:403
  325.2 9.0 %collective-permute-start.11 = (bf16[2,208,1024]{2,1,0:T(8,128)(2,1)}, bf16[2,208,1024]{2,1,0:T(8,128)(2,1)}, u32[]{:S(2)}, u32[]{:S(2)}) collective-permute-start(bf16[2,208,1024]{2,1,0:T(8,128)(2,1)} %collective-permute-done.5.refs_2_), channel_id=1, source_target_pairs={{0,1},{1,0},{2,3},{3,2},{4,5},{5,4},{6,7},{7,6},{8,9},{9,8},{10,11... | collective-permute-start | bytes 2555912 | tf_op jit(solution)/shard_map/ppermute | solution.py:403
  325.6 11.6 %collective-permute-start.6 = (bf16[2,64,3328]{2,1,0:T(8,128)(2,1)}, bf16[2,64,3328]{2,1,0:T(8,128)(2,1)}, u32[]{:S(2)}, u32[]{:S(2)}) collective-permute-start(bf16[2,64,3328]{2,1,0:T(8,128)(2,1)} %get-tuple-element.102.refs_1_), channel_id=1, source_target_pairs={{0,1},{1,0},{2,3},{3,2},{4,5},{5,4},{6,7},{7,6},{8,9},{9,8},{10,11... | collective-permute-start | bytes 2555912 | tf_op jit(solution)/shard_map/ppermute | solution.py:403
  327.3 9.9 %collective-permute-start.7 = (bf16[2,64,3328]{2,1,0:T(8,128)(2,1)}, bf16[2,64,3328]{2,1,0:T(8,128)(2,1)}, u32[]{:S(2)}, u32[]{:S(2)}) collective-permute-start(bf16[2,64,3328]{2,1,0:T(8,128)(2,1)} %get-tuple-element.103.refs_2_), channel_id=1, source_target_pairs={{0,1},{1,0},{2,3},{3,2},{4,5},{5,4},{6,7},{7,6},{8,9},{9,8},{10,11... | collective-permute-start | bytes 2555912 | tf_op jit(solution)/shard_map/ppermute | solution.py:403
  328.6 21.9 %collective-permute-start.2 = (bf16[2,208,1024]{2,1,0:T(8,128)(2,1)}, bf16[2,208,1024]{2,1,0:T(8,128)(2,1)}, u32[]{:S(2)}, u32[]{:S(2)}) collective-permute-start(bf16[2,208,1024]{2,1,0:T(8,128)(2,1)} %collective-permute-done.refs_3_), channel_id=1, source_target_pairs={{0,2},{1,3},{2,4},{3,5},{4,6},{5,7},{6,0},{7,1},{8,10},{9,11},{10,... | collective-permute-start | bytes 2555912 | tf_op jit(solution)/shard_map/ppermute | solution.py:400
  329.8 20.7 %collective-permute-start.3 = (bf16[2,208,1024]{2,1,0:T(8,128)(2,1)}, bf16[2,208,1024]{2,1,0:T(8,128)(2,1)}, u32[]{:S(2)}, u32[]{:S(2)}) collective-permute-start(bf16[2,208,1024]{2,1,0:T(8,128)(2,1)} %collective-permute-done.1.refs_4_), channel_id=1, source_target_pairs={{0,6},{1,7},{2,0},{3,1},{4,2},{5,3},{6,4},{7,5},{8,14},{9,15},{10,... | collective-permute-start | bytes 2555912 | tf_op jit(solution)/shard_map/ppermute | solution.py:400
  350.5 3.4 collective-permute-start.12
  351.5 3.6 collective-permute-start.13

commit v4 on v3

--- a/solution.py
+++ b/solution.py
@@ -336,13 +336,56 @@
         wait()
 
 
-def moved(arrays, steps):
+def relayed(targets, pieces):
+    arrays = list({id(p[1]): p[1] for p in pieces}.values())
+    at = {id(x): n for n, x in enumerate(arrays)}
+    intos = [(n, t) for n, t in enumerate(targets) if not isinstance(t, jax.ShapeDtypeStruct)]
+
+    def body(*refs):
+        take = iter(refs[len(intos) :])
+        srcs, dsts, bufs = ([next(take) for _ in one] for one in (arrays, targets, pieces))
+        sems = next(take)
+        me = lax.axis_index("dp")
+        place = me // CORES, me % CORES
+        ins, outs = [], []
+        for n, (t, x, _, here, there) in enumerate(pieces):
+            ins.append(pltpu.make_async_copy(srcs[at[id(x)]].at[here(*place)], bufs[n], sems.at[n, 0]))
+            outs.append(pltpu.make_async_copy(bufs[n], dsts[t].at[there(*place)], sems.at[n, 1]))
+        for copy in ins:
+            copy.start()
+        for come, go in zip(ins, outs, strict=True):
+            come.wait()
+            go.start()
+        for copy in outs:
+            copy.wait()
+
+    any_space = pl.BlockSpec(memory_space=pl.ANY)
+    return pl.pallas_call(
+        body,
+        out_shape=[jax.ShapeDtypeStruct(t.shape, t.dtype) for t in targets],
+        in_specs=[any_space] * (len(intos) + len(arrays)),
+        out_specs=[any_space] * len(targets),
+        scratch_shapes=[pltpu.VMEM(shape, x.dtype) for _, x, shape, *_ in pieces] + [pltpu.SemaphoreType.DMA((len(pieces), 2))],
+        input_output_aliases={i: n for i, (n, _) in enumerate(intos)},
+        compiler_params=pltpu.CompilerParams(vmem_limit_bytes=VMEM),
+    )(*[t for _, t in intos], *arrays)
+
+
+def moved(arrays, steps, hole):
     def body(*refs):
         for src, dst in zip(refs[: len(arrays)], refs[len(arrays) :], strict=True):
             dst[...] = src[...]
 
-    specs = [pl.BlockSpec((x.shape[0] // steps[0], x.shape[1] // steps[1], x.shape[2]), lambda i, j: (i, j, 0)) for x in arrays]
-    size = sum(x.size * x.dtype.itemsize for x in arrays)
+    def spec(n, x):
+        def at(i, j):
+            if n != hole[0]:
+                return i, j, 0
+            step = jnp.where(j == hole[1], j - 1, j)
+            return i, lax.rem(lax.axis_index("dp") // CORES + step, steps[1]), 0
+
+        return pl.BlockSpec((x.shape[0] // steps[0], x.shape[1] // steps[1], x.shape[2]), at)
+
+    specs = [spec(n, x) for n, x in enumerate(arrays)]
     return pl.pallas_call(
         body,
         out_shape=[jax.ShapeDtypeStruct(x.shape, x.dtype) for x in arrays],
@@ -350,46 +393,20 @@
         in_specs=specs,
         out_specs=specs,
         compiler_params=pltpu.CompilerParams(vmem_limit_bytes=VMEM),
-        cost_estimate=pl.CostEstimate(flops=0, bytes_accessed=2 * size, transcendentals=0),
     )(*arrays)
 
 
-def placed(shape, chips, into, pieces):
-    arrays = [p[0] for p in pieces]
-    count = len(arrays)
-
-    def body(*refs):
-        refs = refs[0 if into is None else 1 :]
-        srcs, dst, bufs, sems = refs[:count], refs[count], refs[count + 1 : -1], refs[-1]
-        me = lax.axis_index("dp")
-        chip, core = me // CORES, me % CORES
-        rows = shape[1] // (chips * CORES)
-        ins, outs = [], []
-        for n, (x, d, other, first) in enumerate(pieces):
+def placed(chips, targets, blocks):
+    def piece(t, x, d, other, first):
+        rows = targets[t].shape[1] // (chips * CORES)
+
+        def there(chip, core):
             base = (lax.rem(chip + d, chips) * CORES + (1 - core if other else core)) * rows + first
-            there = dst.at[:, pl.ds(pl.multiple_of(base, STRIP), x.shape[1])]
-            ins.append(pltpu.make_async_copy(srcs[n], bufs[n], sems.at[n, 0]))
-            outs.append(pltpu.make_async_copy(bufs[n], there, sems.at[n, 1]))
-        for copy in ins:
-            copy.start()
-        for come, go in zip(ins, outs, strict=True):
-            come.wait()
-            go.start()
-        for copy in outs:
-            copy.wait()
-
-    any_space = pl.BlockSpec(memory_space=pl.ANY)
-    size = sum(x.size * x.dtype.itemsize for x in arrays)
-    return pl.pallas_call(
-        body,
-        out_shape=jax.ShapeDtypeStruct(shape, arrays[0].dtype),
-        in_specs=[any_space] * (count + (into is not None)),
-        out_specs=any_space,
-        scratch_shapes=[pltpu.VMEM(x.shape, x.dtype) for x in arrays] + [pltpu.SemaphoreType.DMA((count, 2))],
-        input_output_aliases={} if into is None else {0: 0},
-        compiler_params=pltpu.CompilerParams(vmem_limit_bytes=VMEM),
-        cost_estimate=pl.CostEstimate(flops=0, bytes_accessed=2 * size, transcendentals=0),
-    )(*(() if into is None else (into,)), *arrays)
+            return (slice(None), pl.ds(pl.multiple_of(base, STRIP), x.shape[1]))
+
+        return (t, x, x.shape, lambda chip, core: slice(None), there)
+
+    return relayed(targets, [piece(*one) for one in blocks])
 
 
 def solution(mesh):
@@ -439,29 +456,28 @@
             compiler_params=pltpu.CompilerParams(collective_id=0, has_side_effects=True, vmem_limit_bytes=VMEM),
         )(*terms, *weights, *m, *v)
         new, (own_a, own_b, pair, late_a, late_b), moments = out[: count - 1], out[count - 1 : count - 1 + len(tail)], out[count - 1 + len(tail) :]
-        shape, far, hold = weights[-1].shape, chips // 2, lax.optimization_barrier
-        put = functools.partial(placed, shape, chips)
+        far, hold = chips // 2, lax.optimization_barrier
+        back, down = chips - 1, cut_rows
+        put = functools.partial(placed, chips)
         left_a, right_b = hop(own_a, 1), hop(own_b, -1)
         left_b, right_a = hop(own_b, 1), hop(own_a, -1)
-        results = list(moved([*new, *moments], (layers, chips)))
-        left_a, right_b, own_a, results = hold((left_a, right_b, own_a, results))
+        results = list(moved([*new, *moments], (layers, chips), (count - 2, far)))
+        left_a, right_b, late_a, late_b, results = hold((left_a, right_b, late_a, late_b, results))
         far_a, far_b = hop(left_a, 1), hop(right_b, -1)
-        start = [(own_a, 0, 0, 0), (own_b, 0, 0, cut_rows), (pair, 0, 1, 0), (left_a, chips - 1, 0, 0), (right_b, 1, 0, cut_rows)]
-        whole = put(None, start)
-        left_a, right_b, left_b, right_a, late_a, late_b, whole = hold((left_a, right_b, left_b, right_a, late_a, late_b, whole))
         over = [across(x) for x in (left_a, right_b, left_b, right_a)]
         over_late = across(late_a), across(late_b)
-        whole = put(whole, [(left_b, chips - 1, 0, cut_rows), (right_a, 1, 0, 0)])
-        over, whole = hold((over, whole))
-        whole = put(whole, [(x, d, 1, row) for x, d, row in zip(over, (chips - 1, 1, chips - 1, 1), (0, cut_rows, cut_rows, 0), strict=True)])
-        over_late, whole, results = hold((over_late, whole, results))
-        late = [(x, far, other, row) for other, two in enumerate(((late_a, late_b), over_late)) for x, row in zip(two, (0, far_rows), strict=True)]
-        results[count - 2] = placed(weights[-2].shape, chips, results[count - 2], late)
-        far_a, far_b, whole, results = hold((far_a, far_b, whole, results))
+        near = [(0, own_a, 0, 0, 0), (0, own_b, 0, 0, down), (0, pair, 0, 1, 0), (0, left_a, back, 0, 0), (0, right_b, 1, 0, down)]
+        near += [(0, left_b, back, 0, down), (0, right_a, 1, 0, 0), (1, late_a, far, 0, 0), (1, late_b, far, 0, far_rows)]
+        whole, results[count - 2] = put([jax.ShapeDtypeStruct(weights[-1].shape, bf16), results[count - 2]], near)
+        over, over_late, whole, results = hold((over, over_late, whole, results))
+        near = [(0, over[0], back, 1, 0), (0, over[1], 1, 1, down), (0, over[2], back, 1, down), (0, over[3], 1, 1, 0)]
+        near += [(1, over_late[0], far, 1, 0), (1, over_late[1], far, 1, far_rows)]
+        whole, results[count - 2] = put([whole, results[count - 2]], near)
+        far_a, far_b, whole = hold((far_a, far_b, whole))
         over_far_a, over_far_b = across(far_a), across(far_b)
-        whole = put(whole, [(far_a, far, 0, 0), (far_b, far, 0, cut_rows)])
+        [whole] = put([whole], [(0, far_a, far, 0, 0), (0, far_b, far, 0, down)])
         over_far_a, over_far_b, whole = hold((over_far_a, over_far_b, whole))
-        whole = put(whole, [(over_far_a, far, 1, 0), (over_far_b, far, 1, cut_rows)])
+        [whole] = put([whole], [(0, over_far_a, far, 1, 0), (0, over_far_b, far, 1, down)])
         return (*results[: count - 1], whole, *results[count - 1 :])
 
     all_of, cut = P(None, None, None), P(None, "dp", None)

time: 358 us -> 353 us (0.986)
  Pallas kernels: 333 us -> 329 us
    pallas_call x6 -> x4, Pallas kernels: 17.4 us -> 15.6 us  [relayed(): pl.pallas_call(body, out_shape=[jax.ShapeDtypeStruct(t.shape, t.dtype) fo...]
  transfers between devices with their start and end apart: 14 -> 14, of which waited for: 5 -> 5; matrix products, arithmetic and copies ran while one was open for 0% -> 0% of each run, Pallas kernels for 13% -> 12%
where the time goes in v4:
time: 353 us
  Pallas kernels  329 us (93%)
  waiting for transfers between devices  13.4 us (4%)
  starting transfers between devices  9.21 us (3%)
    pallas_call x1, Pallas kernels, step(): pl.pallas_call(functools.partial(kernel, chips, layers, kinds), out_shape...  285 us
    pallas_call x1, Pallas kernels, moved(): pl.pallas_call(body, out_shape=[jax.ShapeDtypeStruct(x.shape, x.dtype) fo...  28.6 us
    pallas_call x4, Pallas kernels, relayed(): pl.pallas_call(body, out_shape=[jax.ShapeDtypeStruct(t.shape, t.dtype) fo...  15.6 us
    ppermute x6, waiting for transfers between devices, hop(): lax.ppermute(x, 'dp', [(i, (i + d * CORES) % devices) for i in range(devi...  8.29 us
  transfers between devices with their start and end apart: 14, of which 5 were waited for; matrix products, arithmetic and copies ran while one was open for 0% of the time, Pallas kernels for 12%

profile of v4, /device:TPU:113, one launch (start us, length us, event | category | flops | bytes accessed | tf_op | source)
XLA Modules:
  0.0 352.5 jit_solution(11852953593628431561)
XLA Ops:
  0.6 285.0 %shard_map.187 = (bf16[2,1024,3328]{2,1,0:T(8,128)(2,1)}, bf16[2,1024,3328]{2,1,0:T(8,128)(2,1)}, bf16[2,208,1024]{2,1,0:T(8,128)(2,1)}, bf16[2,208,1024]{2,1,0:...) custom-call(bf16[1,2,1024,3328]{3,2,1,0:T(8,128)(2,1)} %refs_0_.1, ...), custom_call_target="tpu_custom_call" | custom-call | tf_op jit(solution)/shard_map/pallas_call | solution.py:437
  285.6 1.0 collective-permute-start
  286.6 1.8 collective-permute-start.1
  288.4 0.0 collective-permute-start.4
  288.4 2.7 collective-permute-start.6
  291.1 28.6 %shard_map.188 = (bf16[2,1024,3328]{2,1,0:T(8,128)(2,1)}, bf16[2,1024,3328]{2,1,0:T(8,128)(2,1)}, f32[2,128,3328]{2,1,0:T(8,128)}, f32[2,128,3328]{2,1,0:T(8,128...) custom-call(bf16[2,1024,3328]{2,1,0:T(8,128)(2,1)} %get-tuple-element., ...), custom_call_target="tpu_custom_call" | custom-call | tf_op jit(solution)/shard_map/pallas_call | solution.py:389
  319.7 0.0 collective-permute-done.refs_4_
  319.7 0.0 collective-permute-done.1.refs_5_
  319.7 0.1 collective-permute-start.2
  319.8 0.5 collective-permute-start.3
  320.3 0.1 collective-permute-start.8
  320.4 0.0 collective-permute-done.4.refs_6_
  320.4 0.4 collective-permute-start.9
  320.8 0.0 collective-permute-done.6.refs_7_
  320.8 0.1 collective-permute-start.5
  320.9 1.6 collective-permute-done.2.refs_2_
  322.5 0.1 collective-permute-start.7
  322.6 1.1 collective-permute-done.3.refs_3_
  323.7 0.0 collective-permute-start.10
  323.7 1.2 collective-permute-done.8.refs_6_
  324.9 1.5 collective-permute-start.11
  326.4 6.5 %shard_map.189 = (bf16[2,3328,1024]{2,1,0:T(8,128)(2,1)}, bf16[2,1024,3328]{2,1,0:T(8,128)(2,1)}) custom-call(bf16[2,1024,3328]{2,1,0:T(8,128)(2,1)} %get-tuple-element.91.refs_0_, bf16[2,208,1024]{2,1,0:T(8,128)(2,1)} %get-tuple-element.67.refs_1_, bf16[2,208,1024]{2,1,0:T(8,128)(2,1)} %get-tuple-element.68.refs_2_, ...), custom_call_target="tpu_custom_call", output_to_operand_aliasing={{1}: (0, {})} | custom-call | tf_op jit(solution)/shard_map/pallas_call | solution.py:363
  332.9 0.0 collective-permute-done.9.refs_7_
  332.9 0.0 collective-permute-done.5.refs_4_
  332.9 0.0 collective-permute-done.7.refs_5_
  333.0 4.4 %shard_map.190 = (bf16[2,3328,1024]{2,1,0:T(8,128)(2,1)}, bf16[2,1024,3328]{2,1,0:T(8,128)(2,1)}) custom-call(bf16[2,3328,1024]{2,1,0:T(8,128)(2,1)} %get-tuple-element.103.refs_0_, bf16[2,1024,3328]{2,1,0:T(8,128)(2,1)} %get-tuple-element.104.refs_1_, ...), custom_call_target="tpu_custom_call", output_to_operand_aliasing={{0}: (0, {}), {1}: (1, {})} | custom-call | tf_op jit(solution)/shard_map/pallas_call | solution.py:363
  337.3 8.3 %collective-permute-done.10.refs_1_ = bf16[2,208,1024]{2,1,0:T(8,128)(2,1)} collective-permute-done((bf16[2,208,1024]{2,1,0:T(8,128)(2,1)}, bf16[2,208,1024]{2,1,0:T(8,128)(2,1)}, u32[]{:S(2)}, u32[]{:S(2)}) %collective-permute-start.10) | collective-permute-done | bytes 852000 | tf_op jit(solution)/shard_map/ppermute | solution.py:417
  345.6 0.0 collective-permute-done.11.refs_2_
  345.6 1.0 collective-permute-start.12
  346.6 0.0 collective-permute-start.13
  346.6 2.4 shard_map.191.refs_0_
  349.0 0.0 collective-permute-done.12.refs_1_
  349.0 1.2 collective-permute-done.13.refs_2_
  350.2 2.4 shard_map.192
Async XLA Ops:
  285.6 34.0 %collective-permute-start = (bf16[2,208,1024]{2,1,0:T(8,128)(2,1)}, bf16[2,208,1024]{2,1,0:T(8,128)(2,1)}, u32[]{:S(2)}, u32[]{:S(2)}) collective-permute-start(bf16[2,208,1024]{2,1,0:T(8,128)(2,1)} %get-tuple-element.67.refs_1_), channel_id=1, source_target_pairs={{0,2},{1,3},{2,4},{3,5},{4,6},{5,7},{6,0},{7,1},{8,10},{9,11},{10,... | collective-permute-start | bytes 2555912 | tf_op jit(solution)/shard_map/ppermute | solution.py:417
  286.6 33.1 %collective-permute-start.1 = (bf16[2,208,1024]{2,1,0:T(8,128)(2,1)}, bf16[2,208,1024]{2,1,0:T(8,128)(2,1)}, u32[]{:S(2)}, u32[]{:S(2)}) collective-permute-start(bf16[2,208,1024]{2,1,0:T(8,128)(2,1)} %get-tuple-element.68.refs_2_), channel_id=1, source_target_pairs={{0,6},{1,7},{2,0},{3,1},{4,2},{5,3},{6,4},{7,5},{8,14},{9,15},{10,... | collective-permute-start | bytes 2555912 | tf_op jit(solution)/shard_map/ppermute | solution.py:417
  288.4 32.0 %collective-permute-start.4 = (bf16[2,208,1024]{2,1,0:T(8,128)(2,1)}, bf16[2,208,1024]{2,1,0:T(8,128)(2,1)}, u32[]{:S(2)}, u32[]{:S(2)}) collective-permute-start(bf16[2,208,1024]{2,1,0:T(8,128)(2,1)} %get-tuple-element.68.refs_2_), channel_id=1, source_target_pairs={{0,2},{1,3},{2,4},{3,5},{4,6},{5,7},{6,0},{7,1},{8,10},{9,11},{10,... | collective-permute-start | bytes 2555912 | tf_op jit(solution)/shard_map/ppermute | solution.py:417
  288.4 32.4 %collective-permute-start.6 = (bf16[2,208,1024]{2,1,0:T(8,128)(2,1)}, bf16[2,208,1024]{2,1,0:T(8,128)(2,1)}, u32[]{:S(2)}, u32[]{:S(2)}) collective-permute-start(bf16[2,208,1024]{2,1,0:T(8,128)(2,1)} %get-tuple-element.67.refs_1_), channel_id=1, source_target_pairs={{0,6},{1,7},{2,0},{3,1},{4,2},{5,3},{6,4},{7,5},{8,14},{9,15},{10,... | collective-permute-start | bytes 2555912 | tf_op jit(solution)/shard_map/ppermute | solution.py:417
  319.7 2.8 collective-permute-start.2
  319.8 3.9 %collective-permute-start.3 = (bf16[2,208,1024]{2,1,0:T(8,128)(2,1)}, bf16[2,208,1024]{2,1,0:T(8,128)(2,1)}, u32[]{:S(2)}, u32[]{:S(2)}) collective-permute-start(bf16[2,208,1024]{2,1,0:T(8,128)(2,1)} %collective-permute-done.1.refs_5_), channel_id=1, source_target_pairs={{0,1},{1,0},{2,3},{3,2},{4,5},{5,4},{6,7},{7,6},{8,9},{9,8},{10,11... | collective-permute-start | bytes 2555912 | tf_op jit(solution)/shard_map/ppermute | solution.py:420
  320.3 4.6 %collective-permute-start.8 = (bf16[2,64,3328]{2,1,0:T(8,128)(2,1)}, bf16[2,64,3328]{2,1,0:T(8,128)(2,1)}, u32[]{:S(2)}, u32[]{:S(2)}) collective-permute-start(bf16[2,64,3328]{2,1,0:T(8,128)(2,1)} %get-tuple-element.89.refs_8_), channel_id=1, source_target_pairs={{0,1},{1,0},{2,3},{3,2},{4,5},{5,4},{6,7},{7,6},{8,9},{9,8},{10,11... | collective-permute-start | bytes 2555912 | tf_op jit(solution)/shard_map/ppermute | solution.py:420
  320.4 12.6 %collective-permute-start.9 = (bf16[2,64,3328]{2,1,0:T(8,128)(2,1)}, bf16[2,64,3328]{2,1,0:T(8,128)(2,1)}, u32[]{:S(2)}, u32[]{:S(2)}) collective-permute-start(bf16[2,64,3328]{2,1,0:T(8,128)(2,1)} %get-tuple-element.90.refs_9_), channel_id=1, source_target_pairs={{0,1},{1,0},{2,3},{3,2},{4,5},{5,4},{6,7},{7,6},{8,9},{9,8},{10,11... | collective-permute-start | bytes 2555912 | tf_op jit(solution)/shard_map/ppermute | solution.py:420
  320.8 12.2 %collective-permute-start.5 = (bf16[2,208,1024]{2,1,0:T(8,128)(2,1)}, bf16[2,208,1024]{2,1,0:T(8,128)(2,1)}, u32[]{:S(2)}, u32[]{:S(2)}) collective-permute-start(bf16[2,208,1024]{2,1,0:T(8,128)(2,1)} %collective-permute-done.4.refs_6_), channel_id=1, source_target_pairs={{0,1},{1,0},{2,3},{3,2},{4,5},{5,4},{6,7},{7,6},{8,9},{9,8},{10,11... | collective-permute-start | bytes 2555912 | tf_op jit(solution)/shard_map/ppermute | solution.py:420
  322.5 10.5 %collective-permute-start.7 = (bf16[2,208,1024]{2,1,0:T(8,128)(2,1)}, bf16[2,208,1024]{2,1,0:T(8,128)(2,1)}, u32[]{:S(2)}, u32[]{:S(2)}) collective-permute-start(bf16[2,208,1024]{2,1,0:T(8,128)(2,1)} %collective-permute-done.6.refs_7_), channel_id=1, source_target_pairs={{0,1},{1,0},{2,3},{3,2},{4,5},{5,4},{6,7},{7,6},{8,9},{9,8},{10,11... | collective-permute-start | bytes 2555912 | tf_op jit(solution)/shard_map/ppermute | solution.py:420
  323.7 21.9 %collective-permute-start.10 = (bf16[2,208,1024]{2,1,0:T(8,128)(2,1)}, bf16[2,208,1024]{2,1,0:T(8,128)(2,1)}, u32[]{:S(2)}, u32[]{:S(2)}) collective-permute-start(bf16[2,208,1024]{2,1,0:T(8,128)(2,1)} %collective-permute-done.refs_4_), channel_id=1, source_target_pairs={{0,2},{1,3},{2,4},{3,5},{4,6},{5,7},{6,0},{7,1},{8,10},{9,11},{10,... | collective-permute-start | bytes 2555912 | tf_op jit(solution)/shard_map/ppermute | solution.py:417
  324.9 20.7 %collective-permute-start.11 = (bf16[2,208,1024]{2,1,0:T(8,128)(2,1)}, bf16[2,208,1024]{2,1,0:T(8,128)(2,1)}, u32[]{:S(2)}, u32[]{:S(2)}) collective-permute-start(bf16[2,208,1024]{2,1,0:T(8,128)(2,1)} %collective-permute-done.1.refs_5_), channel_id=1, source_target_pairs={{0,6},{1,7},{2,0},{3,1},{4,2},{5,3},{6,4},{7,5},{8,14},{9,15},{10,... | collective-permute-start | bytes 2555912 | tf_op jit(solution)/shard_map/ppermute | solution.py:417
  345.6 3.4 collective-permute-start.12
  346.6 3.6 %collective-permute-start.13 = (bf16[2,208,1024]{2,1,0:T(8,128)(2,1)}, bf16[2,208,1024]{2,1,0:T(8,128)(2,1)}, u32[]{:S(2)}, u32[]{:S(2)}) collective-permute-start(bf16[2,208,1024]{2,1,0:T(8,128)(2,1)} %collective-permute-done.11.refs_2_), channel_id=1, source_target_pairs={{0,1},{1,0},{2,3},{3,2},{4,5},{5,4},{6,7},{7,6},{8,9},{9,8},{10,11... | collective-permute-start | bytes 2555912 | tf_op jit(solution)/shard_map/ppermute | solution.py:420

commit v5 on v4

--- a/solution.py
+++ b/solution.py
@@ -336,38 +336,44 @@
         wait()
 
 
-def relayed(targets, pieces):
+def relayed(targets, pieces, near=(), leave=VMEM * 3 // 4):
+    near = {id(x) for x in near}
     arrays = list({id(p[1]): p[1] for p in pieces}.values())
     at = {id(x): n for n, x in enumerate(arrays)}
     intos = [(n, t) for n, t in enumerate(targets) if not isinstance(t, jax.ShapeDtypeStruct)]
+    through, direct = ([p for p in pieces if (id(p[1]) in near) == one] for one in (False, True))
 
     def body(*refs):
         take = iter(refs[len(intos) :])
-        srcs, dsts, bufs = ([next(take) for _ in one] for one in (arrays, targets, pieces))
+        srcs, dsts, bufs = ([next(take) for _ in one] for one in (arrays, targets, through))
         sems = next(take)
         me = lax.axis_index("dp")
         place = me // CORES, me % CORES
         ins, outs = [], []
-        for n, (t, x, _, here, there) in enumerate(pieces):
+        for n, (t, x, _, here, there) in enumerate(through):
             ins.append(pltpu.make_async_copy(srcs[at[id(x)]].at[here(*place)], bufs[n], sems.at[n, 0]))
             outs.append(pltpu.make_async_copy(bufs[n], dsts[t].at[there(*place)], sems.at[n, 1]))
         for copy in ins:
             copy.start()
-        for come, go in zip(ins, outs, strict=True):
+        for n, (t, x, _, here, there) in enumerate(direct):
+            copy = pltpu.make_async_copy(srcs[at[id(x)]].at[here(*place)], dsts[t].at[there(*place)], sems.at[len(through) + n, 1])
+            copy.start()
+            outs.append(copy)
+        for come, go in zip(ins, outs, strict=False):
             come.wait()
             go.start()
         for copy in outs:
             copy.wait()
 
-    any_space = pl.BlockSpec(memory_space=pl.ANY)
+    any_space = pl.BlockSpec(memory_space=pltpu.HBM)
     return pl.pallas_call(
         body,
         out_shape=[jax.ShapeDtypeStruct(t.shape, t.dtype) for t in targets],
-        in_specs=[any_space] * (len(intos) + len(arrays)),
+        in_specs=[any_space] * len(intos) + [pl.BlockSpec(memory_space=pltpu.VMEM) if id(x) in near else any_space for x in arrays],
         out_specs=[any_space] * len(targets),
-        scratch_shapes=[pltpu.VMEM(shape, x.dtype) for _, x, shape, *_ in pieces] + [pltpu.SemaphoreType.DMA((len(pieces), 2))],
+        scratch_shapes=[pltpu.VMEM(shape, x.dtype) for _, x, shape, *_ in through] + [pltpu.SemaphoreType.DMA((len(pieces), 2))],
         input_output_aliases={i: n for i, (n, _) in enumerate(intos)},
-        compiler_params=pltpu.CompilerParams(vmem_limit_bytes=VMEM),
+        compiler_params=pltpu.CompilerParams(vmem_limit_bytes=VMEM - leave),
     )(*[t for _, t in intos], *arrays)
 
 
@@ -396,7 +402,7 @@
     )(*arrays)
 
 
-def placed(chips, targets, blocks):
+def placed(chips, targets, blocks, **options):
     def piece(t, x, d, other, first):
         rows = targets[t].shape[1] // (chips * CORES)
 
@@ -406,7 +412,7 @@
 
         return (t, x, x.shape, lambda chip, core: slice(None), there)
 
-    return relayed(targets, [piece(*one) for one in blocks])
+    return relayed(targets, [piece(*one) for one in blocks], **options)
 
 
 def solution(mesh):
@@ -466,18 +472,19 @@
         far_a, far_b = hop(left_a, 1), hop(right_b, -1)
         over = [across(x) for x in (left_a, right_b, left_b, right_a)]
         over_late = across(late_a), across(late_b)
+        held = sum(x.size * x.dtype.itemsize for x in (*over, *over_late, far_a, far_b)) + 2**18
         near = [(0, own_a, 0, 0, 0), (0, own_b, 0, 0, down), (0, pair, 0, 1, 0), (0, left_a, back, 0, 0), (0, right_b, 1, 0, down)]
         near += [(0, left_b, back, 0, down), (0, right_a, 1, 0, 0), (1, late_a, far, 0, 0), (1, late_b, far, 0, far_rows)]
-        whole, results[count - 2] = put([jax.ShapeDtypeStruct(weights[-1].shape, bf16), results[count - 2]], near)
+        whole, results[count - 2] = put([jax.ShapeDtypeStruct(weights[-1].shape, bf16), results[count - 2]], near, leave=held)
         over, over_late, whole, results = hold((over, over_late, whole, results))
         near = [(0, over[0], back, 1, 0), (0, over[1], 1, 1, down), (0, over[2], back, 1, down), (0, over[3], 1, 1, 0)]
         near += [(1, over_late[0], far, 1, 0), (1, over_late[1], far, 1, far_rows)]
-        whole, results[count - 2] = put([whole, results[count - 2]], near)
+        whole, results[count - 2] = put([whole, results[count - 2]], near, near=[*over, *over_late])
         far_a, far_b, whole = hold((far_a, far_b, whole))
         over_far_a, over_far_b = across(far_a), across(far_b)
-        [whole] = put([whole], [(0, far_a, far, 0, 0), (0, far_b, far, 0, down)])
+        [whole] = put([whole], [(0, far_a, far, 0, 0), (0, far_b, far, 0, down)], near=[far_a, far_b])
         over_far_a, over_far_b, whole = hold((over_far_a, over_far_b, whole))
-        [whole] = put([whole], [(0, over_far_a, far, 1, 0), (0, over_far_b, far, 1, down)])
+        [whole] = put([whole], [(0, over_far_a, far, 1, 0), (0, over_far_b, far, 1, down)], near=[over_far_a, over_far_b])
         return (*results[: count - 1], whole, *results[count - 1 :])
 
     all_of, cut = P(None, None, None), P(None, "dp", None)

time: 353 us -> 351 us (level)
  Pallas kernels: 329 us -> 325 us
    pallas_call x4, Pallas kernels: 15.6 us -> 11.4 us  [relayed(): pl.pallas_call(body, out_shape=[jax.ShapeDtypeStruct(t.shape, t.dtype) fo...]
  transfers between devices with their start and end apart: 14 -> 14, of which waited for: 5 -> 6; matrix products, arithmetic and copies ran while one was open for 0% -> 0% of each run, Pallas kernels for 12% -> 11%
where the time goes in v5:
time: 351 us
  Pallas kernels  325 us (93%)
  waiting for transfers between devices  15.9 us (5%)
  starting transfers between devices  9.21 us (3%)
    pallas_call x1, Pallas kernels, step(): pl.pallas_call(functools.partial(kernel, chips, layers, kinds), out_shape...  285 us
    pallas_call x1, Pallas kernels, moved(): pl.pallas_call(body, out_shape=[jax.ShapeDtypeStruct(x.shape, x.dtype) fo...  28.6 us
    pallas_call x4, Pallas kernels, relayed(): pl.pallas_call(body, out_shape=[jax.ShapeDtypeStruct(t.shape, t.dtype) fo...  11.4 us
    ppermute x6, waiting for transfers between devices, hop(): lax.ppermute(x, 'dp', [(i, (i + d * CORES) % devices) for i in range(devi...  10.1 us
  transfers between devices with their start and end apart: 14, of which 6 were waited for; matrix products, arithmetic and copies ran while one was open for 0% of the time, Pallas kernels for 11%

profile of v5, /device:TPU:113, one launch (start us, length us, event | category | flops | bytes accessed | tf_op | source)
XLA Modules:
  0.0 350.8 jit_solution(2772683925523553393)
XLA Ops:
  0.6 285.0 %shard_map.187 = (bf16[2,1024,3328]{2,1,0:T(8,128)(2,1)}, bf16[2,1024,3328]{2,1,0:T(8,128)(2,1)}, bf16[2,208,1024]{2,1,0:T(8,128)(2,1)}, bf16[2,208,1024]{2,1,0:...) custom-call(bf16[1,2,1024,3328]{3,2,1,0:T(8,128)(2,1)} %refs_0_.1, ...), custom_call_target="tpu_custom_call" | custom-call | tf_op jit(solution)/shard_map/pallas_call | solution.py:443
  285.6 1.0 collective-permute-start
  286.6 1.8 collective-permute-start.1
  288.4 0.0 collective-permute-start.4
  288.4 2.7 collective-permute-start.6
  291.1 28.6 %shard_map.188 = (bf16[2,1024,3328]{2,1,0:T(8,128)(2,1)}, bf16[2,1024,3328]{2,1,0:T(8,128)(2,1)}, f32[2,128,3328]{2,1,0:T(8,128)}, f32[2,128,3328]{2,1,0:T(8,128...) custom-call(bf16[2,1024,3328]{2,1,0:T(8,128)(2,1)} %get-tuple-element., ...), custom_call_target="tpu_custom_call" | custom-call | tf_op jit(solution)/shard_map/pallas_call | solution.py:395
  319.7 0.0 collective-permute-done.refs_4_
  319.7 0.0 collective-permute-done.1.refs_5_
  319.7 0.1 collective-permute-start.2
  319.8 0.5 collective-permute-start.3
  320.3 0.1 collective-permute-start.8
  320.4 0.0 collective-permute-done.4.refs_6_
  320.4 0.4 collective-permute-start.9
  320.8 0.0 collective-permute-done.6.refs_7_
  320.8 0.1 collective-permute-start.5
  320.9 1.5 collective-permute-done.2.refs_2_
  322.3 0.1 collective-permute-start.7
  322.5 1.1 collective-permute-done.3.refs_3_
  323.6 0.0 collective-permute-start.10
  323.6 1.2 collective-permute-done.8.refs_6_
  324.8 1.5 collective-permute-start.11
  326.2 6.5 %shard_map.189 = (bf16[2,3328,1024]{2,1,0:T(8,128)(2,1)}, bf16[2,1024,3328]{2,1,0:T(8,128)(2,1)}) custom-call(bf16[2,1024,3328]{2,1,0:T(8,128)(2,1)} %get-tuple-element.91.refs_0_, bf16[2,208,1024]{2,1,0:T(8,128)(2,1)} %get-tuple-element.67.refs_1_, bf16[2,208,1024]{2,1,0:T(8,128)(2,1)} %get-tuple-element.68.refs_2_, ...), custom_call_target="tpu_custom_call", output_to_operand_aliasing={{1}: (0, {})} | custom-call | tf_op jit(solution)/shard_map/pallas_call | solution.py:369
  332.8 0.0 collective-permute-done.9.refs_7_
  332.8 0.0 collective-permute-done.5.refs_4_
  332.8 0.0 collective-permute-done.7.refs_5_
  332.8 2.4 shard_map.190
  335.3 10.1 %collective-permute-done.10.refs_1_ = bf16[2,208,1024]{2,1,0:T(8,128)(2,1)S(1)} collective-permute-done((bf16[2,208,1024]{2,1,0:T(8,128)(2,1)}, bf16[2,208,1024]{2,1,0:T(8,128)(2,1)S(1)}, u32[]{:S(2)}, u32[]{:S(2)}) %collective-permute-start.10) | collective-permute-done | bytes 852000 | tf_op jit(solution)/shard_map/ppermute | solution.py:423
  345.4 0.0 collective-permute-done.11.refs_2_
  345.4 1.0 collective-permute-start.12
  346.4 0.0 collective-permute-start.13
  346.4 1.2 shard_map.191.refs_0_
  347.6 0.8 collective-permute-done.12.refs_1_
  348.4 1.2 collective-permute-done.13.refs_2_
  349.6 1.2 shard_map.192
Async XLA Ops:
  285.6 34.0 %collective-permute-start = (bf16[2,208,1024]{2,1,0:T(8,128)(2,1)}, bf16[2,208,1024]{2,1,0:T(8,128)(2,1)}, u32[]{:S(2)}, u32[]{:S(2)}) collective-permute-start(bf16[2,208,1024]{2,1,0:T(8,128)(2,1)} %get-tuple-element.67.refs_1_), channel_id=1, source_target_pairs={{0,2},{1,3},{2,4},{3,5},{4,6},{5,7},{6,0},{7,1},{8,10},{9,11},{10,... | collective-permute-start | bytes 2555912 | tf_op jit(solution)/shard_map/ppermute | solution.py:423
  286.6 33.1 %collective-permute-start.1 = (bf16[2,208,1024]{2,1,0:T(8,128)(2,1)}, bf16[2,208,1024]{2,1,0:T(8,128)(2,1)}, u32[]{:S(2)}, u32[]{:S(2)}) collective-permute-start(bf16[2,208,1024]{2,1,0:T(8,128)(2,1)} %get-tuple-element.68.refs_2_), channel_id=1, source_target_pairs={{0,6},{1,7},{2,0},{3,1},{4,2},{5,3},{6,4},{7,5},{8,14},{9,15},{10,... | collective-permute-start | bytes 2555912 | tf_op jit(solution)/shard_map/ppermute | solution.py:423
  288.4 32.0 %collective-permute-start.4 = (bf16[2,208,1024]{2,1,0:T(8,128)(2,1)}, bf16[2,208,1024]{2,1,0:T(8,128)(2,1)}, u32[]{:S(2)}, u32[]{:S(2)}) collective-permute-start(bf16[2,208,1024]{2,1,0:T(8,128)(2,1)} %get-tuple-element.68.refs_2_), channel_id=1, source_target_pairs={{0,2},{1,3},{2,4},{3,5},{4,6},{5,7},{6,0},{7,1},{8,10},{9,11},{10,... | collective-permute-start | bytes 2555912 | tf_op jit(solution)/shard_map/ppermute | solution.py:423
  288.4 32.4 %collective-permute-start.6 = (bf16[2,208,1024]{2,1,0:T(8,128)(2,1)}, bf16[2,208,1024]{2,1,0:T(8,128)(2,1)}, u32[]{:S(2)}, u32[]{:S(2)}) collective-permute-start(bf16[2,208,1024]{2,1,0:T(8,128)(2,1)} %get-tuple-element.67.refs_1_), channel_id=1, source_target_pairs={{0,6},{1,7},{2,0},{3,1},{4,2},{5,3},{6,4},{7,5},{8,14},{9,15},{10,... | collective-permute-start | bytes 2555912 | tf_op jit(solution)/shard_map/ppermute | solution.py:423
  319.7 2.7 collective-permute-start.2
  319.8 3.8 %collective-permute-start.3 = (bf16[2,208,1024]{2,1,0:T(8,128)(2,1)}, bf16[2,208,1024]{2,1,0:T(8,128)(2,1)S(1)}, u32[]{:S(2)}, u32[]{:S(2)}) collective-permute-start(bf16[2,208,1024]{2,1,0:T(8,128)(2,1)} %collective-permute-done.1.refs_5_), channel_id=1, source_target_pairs={{0,1},{1,0},{2,3},{3,2},{4,5},{5,4},{6,7},{7,6},{8,9},{9,8},{10,11... | collective-permute-start | bytes 2555912 | tf_op jit(solution)/shard_map/ppermute | solution.py:426
  320.3 4.5 %collective-permute-start.8 = (bf16[2,64,3328]{2,1,0:T(8,128)(2,1)}, bf16[2,64,3328]{2,1,0:T(8,128)(2,1)S(1)}, u32[]{:S(2)}, u32[]{:S(2)}) collective-permute-start(bf16[2,64,3328]{2,1,0:T(8,128)(2,1)} %get-tuple-element.89.refs_8_), channel_id=1, source_target_pairs={{0,1},{1,0},{2,3},{3,2},{4,5},{5,4},{6,7},{7,6},{8,9},{9,8},{10,11... | collective-permute-start | bytes 2555912 | tf_op jit(solution)/shard_map/ppermute | solution.py:426
  320.4 12.4 %collective-permute-start.9 = (bf16[2,64,3328]{2,1,0:T(8,128)(2,1)}, bf16[2,64,3328]{2,1,0:T(8,128)(2,1)S(1)}, u32[]{:S(2)}, u32[]{:S(2)}) collective-permute-start(bf16[2,64,3328]{2,1,0:T(8,128)(2,1)} %get-tuple-element.90.refs_9_), channel_id=1, source_target_pairs={{0,1},{1,0},{2,3},{3,2},{4,5},{5,4},{6,7},{7,6},{8,9},{9,8},{10,11... | collective-permute-start | bytes 2555912 | tf_op jit(solution)/shard_map/ppermute | solution.py:426
  320.8 12.0 %collective-permute-start.5 = (bf16[2,208,1024]{2,1,0:T(8,128)(2,1)}, bf16[2,208,1024]{2,1,0:T(8,128)(2,1)S(1)}, u32[]{:S(2)}, u32[]{:S(2)}) collective-permute-start(bf16[2,208,1024]{2,1,0:T(8,128)(2,1)} %collective-permute-done.4.refs_6_), channel_id=1, source_target_pairs={{0,1},{1,0},{2,3},{3,2},{4,5},{5,4},{6,7},{7,6},{8,9},{9,8},{10,11... | collective-permute-start | bytes 2555912 | tf_op jit(solution)/shard_map/ppermute | solution.py:426
  322.3 10.5 %collective-permute-start.7 = (bf16[2,208,1024]{2,1,0:T(8,128)(2,1)}, bf16[2,208,1024]{2,1,0:T(8,128)(2,1)S(1)}, u32[]{:S(2)}, u32[]{:S(2)}) collective-permute-start(bf16[2,208,1024]{2,1,0:T(8,128)(2,1)} %collective-permute-done.6.refs_7_), channel_id=1, source_target_pairs={{0,1},{1,0},{2,3},{3,2},{4,5},{5,4},{6,7},{7,6},{8,9},{9,8},{10,11... | collective-permute-start | bytes 2555912 | tf_op jit(solution)/shard_map/ppermute | solution.py:426
  323.6 21.8 %collective-permute-start.10 = (bf16[2,208,1024]{2,1,0:T(8,128)(2,1)}, bf16[2,208,1024]{2,1,0:T(8,128)(2,1)S(1)}, u32[]{:S(2)}, u32[]{:S(2)}) collective-permute-start(bf16[2,208,1024]{2,1,0:T(8,128)(2,1)} %collective-permute-done.refs_4_), channel_id=1, source_target_pairs={{0,2},{1,3},{2,4},{3,5},{4,6},{5,7},{6,0},{7,1},{8,10},{9,11},{10,... | collective-permute-start | bytes 2555912 | tf_op jit(solution)/shard_map/ppermute | solution.py:423
  324.8 20.6 %collective-permute-start.11 = (bf16[2,208,1024]{2,1,0:T(8,128)(2,1)}, bf16[2,208,1024]{2,1,0:T(8,128)(2,1)S(1)}, u32[]{:S(2)}, u32[]{:S(2)}) collective-permute-start(bf16[2,208,1024]{2,1,0:T(8,128)(2,1)} %collective-permute-done.1.refs_5_), channel_id=1, source_target_pairs={{0,6},{1,7},{2,0},{3,1},{4,2},{5,3},{6,4},{7,5},{8,14},{9,15},{10,... | collective-permute-start | bytes 2555912 | tf_op jit(solution)/shard_map/ppermute | solution.py:423
  345.4 3.0 collective-permute-start.12
  346.4 3.2 collective-permute-start.13

commit v6 on v5

--- a/solution.py
+++ b/solution.py
@@ -48,6 +48,10 @@
     turn = [lax.rem(chip + d, chips) for d in range(chips)]
     right, left = turn[1] * CORES + core, turn[chips - 1] * CORES + core
     far = chips // 2
+
+    barrier = pltpu.get_barrier_semaphore()
+    for other in (left, right, partner):
+        pl.semaphore_signal(barrier, inc=1, device_id={"dp": other}, device_id_type=MESH)
 
     chunks = [(a, layer) for a in range(count) for layer in range(layers)]
     rows = [r.shape[2] for r in part]
@@ -319,9 +323,6 @@
             if chunks[j][0] != last - 1:
                 go(j, then)
 
-    barrier = pltpu.get_barrier_semaphore()
-    for other in (partner, right, left):
-        pl.semaphore_signal(barrier, inc=1, device_id={"dp": other}, device_id_type=MESH)
     pl.semaphore_wait(barrier, 3)
 
     acts = {"pair": start_pair, "follow": follow, "lead": lead, "first": first, "middle": middle, "final": final, "pass": pass_on, "hand": hand_over}
@@ -480,11 +481,15 @@
         near = [(0, over[0], back, 1, 0), (0, over[1], 1, 1, down), (0, over[2], back, 1, down), (0, over[3], 1, 1, 0)]
         near += [(1, over_late[0], far, 1, 0), (1, over_late[1], far, 1, far_rows)]
         whole, results[count - 2] = put([whole, results[count - 2]], near, near=[*over, *over_late])
-        far_a, far_b, whole = hold((far_a, far_b, whole))
-        over_far_a, over_far_b = across(far_a), across(far_b)
+        far_a, whole = hold((far_a, whole))
+        over_far_a = across(far_a)
+        far_b, whole = hold((far_b, whole))
+        over_far_b = across(far_b)
         [whole] = put([whole], [(0, far_a, far, 0, 0), (0, far_b, far, 0, down)], near=[far_a, far_b])
-        over_far_a, over_far_b, whole = hold((over_far_a, over_far_b, whole))
-        [whole] = put([whole], [(0, over_far_a, far, 1, 0), (0, over_far_b, far, 1, down)], near=[over_far_a, over_far_b])
+        over_far_a, whole = hold((over_far_a, whole))
+        [whole] = put([whole], [(0, over_far_a, far, 1, 0)], near=[over_far_a])
+        over_far_b, whole = hold((over_far_b, whole))
+        [whole] = put([whole], [(0, over_far_b, far, 1, down)], near=[over_far_b])
         return (*results[: count - 1], whole, *results[count - 1 :])
 
     all_of, cut = P(None, None, None), P(None, "dp", None)

time: 351 us -> 351 us (level)
    pallas_call x4 -> x5, Pallas kernels: 11.4 us -> 12 us  [relayed(): pl.pallas_call(body, out_shape=[jax.ShapeDtypeStruct(t.shape, t.dtype) fo...]
where the time goes in v6:
time: 351 us; the launch traced here: 350 us
  Pallas kernels  326 us (93%)
  waiting for transfers between devices  14.9 us (4%)
  starting transfers between devices  9.21 us (3%)
    pallas_call x1, Pallas kernels, step(): pl.pallas_call(functools.partial(kernel, chips, layers, kinds), out_shape...  285 us
    pallas_call x1, Pallas kernels, moved(): pl.pallas_call(body, out_shape=[jax.ShapeDtypeStruct(x.shape, x.dtype) fo...  28.6 us
    pallas_call x5, Pallas kernels, relayed(): pl.pallas_call(body, out_shape=[jax.ShapeDtypeStruct(t.shape, t.dtype) fo...  12 us
    ppermute x6, waiting for transfers between devices, hop(): lax.ppermute(x, 'dp', [(i, (i + d * CORES) % devices) for i in range(devi...  10.1 us
  transfers between devices with their start and end apart: 14, of which 6 were waited for; matrix products, arithmetic and copies ran while one was open for 0% of the time, Pallas kernels for 11%

profile of v6, /device:TPU:113, one launch (start us, length us, event | category | flops | bytes accessed | tf_op | source)
XLA Modules:
  0.0 350.5 jit_solution(18270941659815019638)
XLA Ops:
  0.6 285.0 %shard_map.187 = (bf16[2,1024,3328]{2,1,0:T(8,128)(2,1)}, bf16[2,1024,3328]{2,1,0:T(8,128)(2,1)}, bf16[2,208,1024]{2,1,0:T(8,128)(2,1)}, bf16[2,208,1024]{2,1,0:...) custom-call(bf16[1,2,1024,3328]{3,2,1,0:T(8,128)(2,1)} %refs_0_.1, ...), custom_call_target="tpu_custom_call" | custom-call | tf_op jit(solution)/shard_map/pallas_call | solution.py:444
  285.6 0.9 collective-permute-start
  286.5 1.8 collective-permute-start.1
  288.4 0.0 collective-permute-start.4
  288.4 2.7 collective-permute-start.6
  291.0 28.6 %shard_map.188 = (bf16[2,1024,3328]{2,1,0:T(8,128)(2,1)}, bf16[2,1024,3328]{2,1,0:T(8,128)(2,1)}, f32[2,128,3328]{2,1,0:T(8,128)}, f32[2,128,3328]{2,1,0:T(8,128...) custom-call(bf16[2,1024,3328]{2,1,0:T(8,128)(2,1)} %get-tuple-element., ...), custom_call_target="tpu_custom_call" | custom-call | tf_op jit(solution)/shard_map/pallas_call | solution.py:396
  319.7 0.0 collective-permute-done.refs_4_
  319.7 0.0 collective-permute-done.1.refs_5_
  319.7 0.1 collective-permute-start.2
  319.8 0.5 collective-permute-start.3
  320.3 0.1 collective-permute-start.8
  320.4 0.0 collective-permute-done.4.refs_6_
  320.4 0.4 collective-permute-start.9
  320.8 0.0 collective-permute-done.6.refs_7_
  320.8 0.1 collective-permute-start.5
  320.9 1.5 collective-permute-done.2.refs_2_
  322.3 0.1 collective-permute-start.7
  322.5 1.1 collective-permute-done.3.refs_3_
  323.6 0.0 collective-permute-start.11
  323.6 1.2 collective-permute-done.8.refs_6_
  324.8 1.5 collective-permute-start.10
  326.2 6.5 %shard_map.189 = (bf16[2,3328,1024]{2,1,0:T(8,128)(2,1)}, bf16[2,1024,3328]{2,1,0:T(8,128)(2,1)}) custom-call(bf16[2,1024,3328]{2,1,0:T(8,128)(2,1)} %get-tuple-element.93.refs_0_, bf16[2,208,1024]{2,1,0:T(8,128)(2,1)} %get-tuple-element.69.refs_1_, bf16[2,208,1024]{2,1,0:T(8,128)(2,1)} %get-tuple-element.70.refs_2_, ...), custom_call_target="tpu_custom_call", output_to_operand_aliasing={{1}: (0, {})} | custom-call | tf_op jit(solution)/shard_map/pallas_call | solution.py:370
  332.8 0.0 collective-permute-done.9.refs_7_
  332.8 0.0 collective-permute-done.5.refs_4_
  332.8 0.0 collective-permute-done.7.refs_5_
  332.8 2.4 shard_map.190
  335.3 10.1 %collective-permute-done.11.refs_1_ = bf16[2,208,1024]{2,1,0:T(8,128)(2,1)S(1)} collective-permute-done((bf16[2,208,1024]{2,1,0:T(8,128)(2,1)}, bf16[2,208,1024]{2,1,0:T(8,128)(2,1)S(1)}, u32[]{:S(2)}, u32[]{:S(2)}) %collective-permute-start.11) | collective-permute-done | bytes 852000 | tf_op jit(solution)/shard_map/ppermute | solution.py:424
  345.3 1.0 collective-permute-start.13
  346.3 0.0 collective-permute-done.10.refs_2_
  346.3 0.0 collective-permute-start.12
  346.3 1.2 shard_map.191.refs_0_
  347.6 0.8 collective-permute-done.13.refs_1_
  348.3 0.9 shard_map.192.refs_0_
  349.3 0.3 collective-permute-done.12.refs_1_
  349.6 0.9 shard_map.193
Async XLA Ops:
  285.6 34.0 %collective-permute-start = (bf16[2,208,1024]{2,1,0:T(8,128)(2,1)}, bf16[2,208,1024]{2,1,0:T(8,128)(2,1)}, u32[]{:S(2)}, u32[]{:S(2)}) collective-permute-start(bf16[2,208,1024]{2,1,0:T(8,128)(2,1)} %get-tuple-element.69.refs_1_), channel_id=1, source_target_pairs={{0,2},{1,3},{2,4},{3,5},{4,6},{5,7},{6,0},{7,1},{8,10},{9,11},{10,... | collective-permute-start | bytes 2555912 | tf_op jit(solution)/shard_map/ppermute | solution.py:424
  286.5 33.1 %collective-permute-start.1 = (bf16[2,208,1024]{2,1,0:T(8,128)(2,1)}, bf16[2,208,1024]{2,1,0:T(8,128)(2,1)}, u32[]{:S(2)}, u32[]{:S(2)}) collective-permute-start(bf16[2,208,1024]{2,1,0:T(8,128)(2,1)} %get-tuple-element.70.refs_2_), channel_id=1, source_target_pairs={{0,6},{1,7},{2,0},{3,1},{4,2},{5,3},{6,4},{7,5},{8,14},{9,15},{10,... | collective-permute-start | bytes 2555912 | tf_op jit(solution)/shard_map/ppermute | solution.py:424
  288.4 32.0 %collective-permute-start.4 = (bf16[2,208,1024]{2,1,0:T(8,128)(2,1)}, bf16[2,208,1024]{2,1,0:T(8,128)(2,1)}, u32[]{:S(2)}, u32[]{:S(2)}) collective-permute-start(bf16[2,208,1024]{2,1,0:T(8,128)(2,1)} %get-tuple-element.70.refs_2_), channel_id=1, source_target_pairs={{0,2},{1,3},{2,4},{3,5},{4,6},{5,7},{6,0},{7,1},{8,10},{9,11},{10,... | collective-permute-start | bytes 2555912 | tf_op jit(solution)/shard_map/ppermute | solution.py:424
  288.4 32.4 %collective-permute-start.6 = (bf16[2,208,1024]{2,1,0:T(8,128)(2,1)}, bf16[2,208,1024]{2,1,0:T(8,128)(2,1)}, u32[]{:S(2)}, u32[]{:S(2)}) collective-permute-start(bf16[2,208,1024]{2,1,0:T(8,128)(2,1)} %get-tuple-element.69.refs_1_), channel_id=1, source_target_pairs={{0,6},{1,7},{2,0},{3,1},{4,2},{5,3},{6,4},{7,5},{8,14},{9,15},{10,... | collective-permute-start | bytes 2555912 | tf_op jit(solution)/shard_map/ppermute | solution.py:424
  319.7 2.7 collective-permute-start.2
  319.8 3.8 %collective-permute-start.3 = (bf16[2,208,1024]{2,1,0:T(8,128)(2,1)}, bf16[2,208,1024]{2,1,0:T(8,128)(2,1)S(1)}, u32[]{:S(2)}, u32[]{:S(2)}) collective-permute-start(bf16[2,208,1024]{2,1,0:T(8,128)(2,1)} %collective-permute-done.1.refs_5_), channel_id=1, source_target_pairs={{0,1},{1,0},{2,3},{3,2},{4,5},{5,4},{6,7},{7,6},{8,9},{9,8},{10,11... | collective-permute-start | bytes 2555912 | tf_op jit(solution)/shard_map/ppermute | solution.py:427
  320.3 4.5 %collective-permute-start.8 = (bf16[2,64,3328]{2,1,0:T(8,128)(2,1)}, bf16[2,64,3328]{2,1,0:T(8,128)(2,1)S(1)}, u32[]{:S(2)}, u32[]{:S(2)}) collective-permute-start(bf16[2,64,3328]{2,1,0:T(8,128)(2,1)} %get-tuple-element.91.refs_8_), channel_id=1, source_target_pairs={{0,1},{1,0},{2,3},{3,2},{4,5},{5,4},{6,7},{7,6},{8,9},{9,8},{10,11... | collective-permute-start | bytes 2555912 | tf_op jit(solution)/shard_map/ppermute | solution.py:427
  320.4 12.4 %collective-permute-start.9 = (bf16[2,64,3328]{2,1,0:T(8,128)(2,1)}, bf16[2,64,3328]{2,1,0:T(8,128)(2,1)S(1)}, u32[]{:S(2)}, u32[]{:S(2)}) collective-permute-start(bf16[2,64,3328]{2,1,0:T(8,128)(2,1)} %get-tuple-element.92.refs_9_), channel_id=1, source_target_pairs={{0,1},{1,0},{2,3},{3,2},{4,5},{5,4},{6,7},{7,6},{8,9},{9,8},{10,11... | collective-permute-start | bytes 2555912 | tf_op jit(solution)/shard_map/ppermute | solution.py:427
  320.8 12.0 %collective-permute-start.5 = (bf16[2,208,1024]{2,1,0:T(8,128)(2,1)}, bf16[2,208,1024]{2,1,0:T(8,128)(2,1)S(1)}, u32[]{:S(2)}, u32[]{:S(2)}) collective-permute-start(bf16[2,208,1024]{2,1,0:T(8,128)(2,1)} %collective-permute-done.4.refs_6_), channel_id=1, source_target_pairs={{0,1},{1,0},{2,3},{3,2},{4,5},{5,4},{6,7},{7,6},{8,9},{9,8},{10,11... | collective-permute-start | bytes 2555912 | tf_op jit(solution)/shard_map/ppermute | solution.py:427
  322.3 10.5 %collective-permute-start.7 = (bf16[2,208,1024]{2,1,0:T(8,128)(2,1)}, bf16[2,208,1024]{2,1,0:T(8,128)(2,1)S(1)}, u32[]{:S(2)}, u32[]{:S(2)}) collective-permute-start(bf16[2,208,1024]{2,1,0:T(8,128)(2,1)} %collective-permute-done.6.refs_7_), channel_id=1, source_target_pairs={{0,1},{1,0},{2,3},{3,2},{4,5},{5,4},{6,7},{7,6},{8,9},{9,8},{10,11... | collective-permute-start | bytes 2555912 | tf_op jit(solution)/shard_map/ppermute | solution.py:427
  323.6 21.8 %collective-permute-start.11 = (bf16[2,208,1024]{2,1,0:T(8,128)(2,1)}, bf16[2,208,1024]{2,1,0:T(8,128)(2,1)S(1)}, u32[]{:S(2)}, u32[]{:S(2)}) collective-permute-start(bf16[2,208,1024]{2,1,0:T(8,128)(2,1)} %collective-permute-done.refs_4_), channel_id=1, source_target_pairs={{0,2},{1,3},{2,4},{3,5},{4,6},{5,7},{6,0},{7,1},{8,10},{9,11},{10,... | collective-permute-start | bytes 2555912 | tf_op jit(solution)/shard_map/ppermute | solution.py:424
  324.8 21.6 %collective-permute-start.10 = (bf16[2,208,1024]{2,1,0:T(8,128)(2,1)}, bf16[2,208,1024]{2,1,0:T(8,128)(2,1)S(1)}, u32[]{:S(2)}, u32[]{:S(2)}) collective-permute-start(bf16[2,208,1024]{2,1,0:T(8,128)(2,1)} %collective-permute-done.1.refs_5_), channel_id=1, source_target_pairs={{0,6},{1,7},{2,0},{3,1},{4,2},{5,3},{6,4},{7,5},{8,14},{9,15},{10,... | collective-permute-start | bytes 2555912 | tf_op jit(solution)/shard_map/ppermute | solution.py:424
  345.3 3.0 collective-permute-start.13
  346.3 3.2 collective-permute-start.12

commit v7 on v6

--- a/solution.py
+++ b/solution.py
@@ -15,6 +15,7 @@
 SLOTS = 6
 VMEM = 67043328
 LEAD = 0
+LAST = 16
 SETS = 3
 
 
@@ -37,10 +38,11 @@
     g, w, m, v = ([next(take) for _ in range(count)] for _ in range(4))
     w_out = [next(take) for _ in range(last)]
     new_half, new_pair, far_half = [next(take) for _ in range(2)], next(take), [next(take) for _ in range(2)]
+    to_pass = [next(take) for _ in range(2)]
     m_out, v_out, part, arrived = ([next(take) for _ in range(count)] for _ in range(4))
     shapes = max(kinds) + 1
     own, m_set, v_set, w_set = ([next(take) for _ in range(shapes)] for _ in range(4))
-    own_sem, set_in, set_out, pair_send, pair_recv, ring_send, ring_recv, gather_send, gather_recv, local_sem, early_pair_send, early_pair_recv, early_ring_send, early_ring_recv, turn_sem = take
+    own_sem, set_in, set_out, pair_send, pair_recv, ring_send, ring_recv, gather_send, gather_recv, local_sem, early_pair_send, early_pair_recv, early_ring_send, early_ring_recv, turn_sem, pass_sem = take
 
     me = lax.axis_index("dp")
     chip, core = me // CORES, me % CORES
@@ -262,11 +264,10 @@
             copy.start()
         start_set(q, i + SETS - 1)
 
-    def block(a, layer, chip_of, core_of, h=None):
-        base = (chip_of * CORES + core_of) * rows[a]
-        if h is None:
-            return w_out[a].at[layer, pl.ds(pl.multiple_of(base, STRIP), rows[a])]
-        return w_out[a].at[layer, pl.ds(pl.multiple_of(base + h * half[a], STRIP), half[a])]
+    def block(a, layer, chip_of, core_of, h=None, start=0, end=None):
+        base = (chip_of * CORES + core_of) * rows[a] + (0 if h is None else h * half[a]) + start
+        size = (rows[a] if h is None else half[a]) if end is None else end
+        return w_out[a].at[layer, pl.ds(pl.multiple_of(base, STRIP), size - start)]
 
     def gather_copy(j, n):
         a, layer = chunks[j]
@@ -277,8 +278,9 @@
             return remote(mine(h), block(a, layer, chip, core, h), *s, to)
         if n < 6:
             d, h, to = ((chips - 1, 0, right), (1, 1, left))[n - 4]
-            there = block(a, layer, turn[d], core, h)
-            return remote(there, far_half[h].at[layer] if a == last - 1 else there, *s, to)
+            skip = LAST if j == gathered[-1] else 0
+            there = block(a, layer, turn[d], core, h, skip)
+            return remote(there, far_half[h].at[layer, pl.ds(skip, half[a] - skip)] if a == last - 1 else there, *s, to)
         if n == 6:
             return remote(part[a].at[layer, 0], block(a, layer, chip, core), *s, partner)
         d, h = ((chips - 1, None), (1, None), (far, 0), (far, 1))[n - 7]
@@ -308,10 +310,12 @@
         finish_later(pltpu.make_async_copy(part[a].at[layer, 0], block(a, layer, chip, core), local_sem.at[j, 0]), "wait")
 
     def pass_on(j):
-        gather_copy(j, 0).wait_recv()
-        go(j, 4)
-        gather_copy(j, 3).wait_recv()
-        go(j, 5)
+        a, layer = chunks[j]
+        for n, then, d, h in ((0, 4, chips - 1, 0), (3, 5, 1, 1)):
+            gather_copy(j, n).wait_recv()
+            go(j, then)
+            if j == gathered[-1]:
+                finish_later(pltpu.make_async_copy(block(a, layer, turn[d], core, h, 0, LAST), to_pass[h].at[0], pass_sem.at[h]), "wait")
         gather_copy(j, 1).wait_recv()
         go(j, 7)
         gather_copy(j, 2).wait_recv()
@@ -409,7 +413,8 @@
 
         def there(chip, core):
             base = (lax.rem(chip + d, chips) * CORES + (1 - core if other else core)) * rows + first
-            return (slice(None), pl.ds(pl.multiple_of(base, STRIP), x.shape[1]))
+            layers = targets[t].shape[0]
+            return (pl.ds(layers - x.shape[0], x.shape[0]), pl.ds(pl.multiple_of(base, STRIP), x.shape[1]))
 
         return (t, x, x.shape, lambda chip, core: slice(None), there)
 
@@ -439,7 +444,7 @@
         cut_rows = blocks[-1][0] // 2
         dma = pltpu.SemaphoreType.DMA
         cut_cols, (far_rows, far_cols) = blocks[-1][1], (blocks[-2][0] // 2, blocks[-2][1])
-        tail = [(layers, cut_rows, cut_cols)] * 2 + [(layers, *blocks[-1])] + [(layers, far_rows, far_cols)] * 2
+        tail = [(layers, cut_rows, cut_cols)] * 2 + [(layers, *blocks[-1])] + [(layers, far_rows, far_cols)] * 2 + [(1, LAST, far_cols)] * 2
         early = (2, blocks[0][0] // 2 // STRIP)
         out = pl.pallas_call(
             functools.partial(kernel, chips, layers, kinds),
@@ -459,21 +464,22 @@
             + [dma((chunks, 11))] * 2
             + [dma((chunks, 2))]
             + [dma(early)] * 4
-            + [pltpu.SemaphoreType.REGULAR],
+            + [pltpu.SemaphoreType.REGULAR, dma((2,))],
             compiler_params=pltpu.CompilerParams(collective_id=0, has_side_effects=True, vmem_limit_bytes=VMEM),
         )(*terms, *weights, *m, *v)
-        new, (own_a, own_b, pair, late_a, late_b), moments = out[: count - 1], out[count - 1 : count - 1 + len(tail)], out[count - 1 + len(tail) :]
+        new, (own_a, own_b, pair, late_a, late_b, last_a, last_b), moments = out[: count - 1], out[count - 1 : count - 1 + len(tail)], out[count - 1 + len(tail) :]
         far, hold = chips // 2, lax.optimization_barrier
         back, down = chips - 1, cut_rows
         put = functools.partial(placed, chips)
         left_a, right_b = hop(own_a, 1), hop(own_b, -1)
         left_b, right_a = hop(own_b, 1), hop(own_a, -1)
         results = list(moved([*new, *moments], (layers, chips), (count - 2, far)))
-        left_a, right_b, late_a, late_b, results = hold((left_a, right_b, late_a, late_b, results))
+        left_a, right_b, late_a, late_b, last_a, last_b, results = hold((left_a, right_b, late_a, late_b, last_a, last_b, results))
         far_a, far_b = hop(left_a, 1), hop(right_b, -1)
+        last_a, last_b = hop(last_a, 1), hop(last_b, -1)
         over = [across(x) for x in (left_a, right_b, left_b, right_a)]
         over_late = across(late_a), across(late_b)
-        held = sum(x.size * x.dtype.itemsize for x in (*over, *over_late, far_a, far_b)) + 2**18
+        held = sum(x.size * x.dtype.itemsize for x in (*over, *over_late, far_a, far_b, last_a, last_b)) + 2**18
         near = [(0, own_a, 0, 0, 0), (0, own_b, 0, 0, down), (0, pair, 0, 1, 0), (0, left_a, back, 0, 0), (0, right_b, 1, 0, down)]
         near += [(0, left_b, back, 0, down), (0, right_a, 1, 0, 0), (1, late_a, far, 0, 0), (1, late_b, far, 0, far_rows)]
         whole, results[count - 2] = put([jax.ShapeDtypeStruct(weights[-1].shape, bf16), results[count - 2]], near, leave=held)
@@ -486,10 +492,14 @@
         far_b, whole = hold((far_b, whole))
         over_far_b = across(far_b)
         [whole] = put([whole], [(0, far_a, far, 0, 0), (0, far_b, far, 0, down)], near=[far_a, far_b])
+        last_a, last_b, whole = hold((last_a, last_b, whole))
+        over_last_a, over_last_b = across(last_a), across(last_b)
         over_far_a, whole = hold((over_far_a, whole))
-        [whole] = put([whole], [(0, over_far_a, far, 1, 0)], near=[over_far_a])
-        over_far_b, whole = hold((over_far_b, whole))
-        [whole] = put([whole], [(0, over_far_b, far, 1, down)], near=[over_far_b])
+        some = [(0, over_far_a, far, 1, 0), (1, last_a, far, 0, 0), (1, last_b, far, 0, far_rows)]
+        whole, results[count - 2] = put([whole, results[count - 2]], some, near=[over_far_a, last_a, last_b])
+        over_far_b, over_last_a, over_last_b, whole, results = hold((over_far_b, over_last_a, over_last_b, whole, results))
+        some = [(0, over_far_b, far, 1, down), (1, over_last_a, far, 1, 0), (1, over_last_b, far, 1, far_rows)]
+        whole, results[count - 2] = put([whole, results[count - 2]], some, near=[over_far_b, over_last_a, over_last_b])
         return (*results[: count - 1], whole, *results[count - 1 :])
 
     all_of, cut = P(None, None, None), P(None, "dp", None)

time: 351 us -> 353 us (level)
  starting transfers between devices: 9.21 us -> 13.2 us
    ppermute x6 -> x8, starting transfers between devices: 6.9 us -> 9.64 us  [hop(): lax.ppermute(x, 'dp', [(i, (i + d * CORES) % devices) for i in range(devi...]
    ppermute x6 -> x8, waiting for transfers between devices: 10.1 us -> 11.6 us  [hop(): lax.ppermute(x, 'dp', [(i, (i + d * CORES) % devices) for i in range(devi...]
  transfers between devices with their start and end apart: 14 -> 18, of which waited for: 6 -> 7; matrix products, arithmetic and copies ran while one was open for 0% -> 0% of each run, Pallas kernels for 11% -> 11%
where the time goes in v7:
time: 353 us
  Pallas kernels  324 us (92%)
  waiting for transfers between devices  15.5 us (4%)
  starting transfers between devices  13.2 us (4%)
    pallas_call x1, Pallas kernels, step(): pl.pallas_call(functools.partial(kernel, chips, layers, kinds), out_shape...  283 us
    pallas_call x1, Pallas kernels, moved(): pl.pallas_call(body, out_shape=[jax.ShapeDtypeStruct(x.shape, x.dtype) fo...  28.6 us
    pallas_call x5, Pallas kernels, relayed(): pl.pallas_call(body, out_shape=[jax.ShapeDtypeStruct(t.shape, t.dtype) fo...  12.2 us
    ppermute x8, waiting for transfers between devices, hop(): lax.ppermute(x, 'dp', [(i, (i + d * CORES) % devices) for i in range(devi...  11.6 us
    ppermute x8, starting transfers between devices, hop(): lax.ppermute(x, 'dp', [(i, (i + d * CORES) % devices) for i in range(devi...  9.64 us
  transfers between devices with their start and end apart: 18, of which 7 were waited for; matrix products, arithmetic and copies ran while one was open for 0% of the time, Pallas kernels for 11%

profile of v7, /device:TPU:113, one launch (start us, length us, event | category | flops | bytes accessed | tf_op | source)
XLA Modules:
  0.0 353.1 jit_solution(42907216095545642)
XLA Ops:
  0.6 282.7 %shard_map.187 = (bf16[2,1024,3328]{2,1,0:T(8,128)(2,1)}, bf16[2,1024,3328]{2,1,0:T(8,128)(2,1)}, bf16[2,208,1024]{2,1,0:T(8,128)(2,1)}, bf16[2,208,1024]{2,1,0:...) custom-call(bf16[1,2,1024,3328]{3,2,1,0:T(8,128)(2,1)} %refs_0_.1, ...), custom_call_target="tpu_custom_call" | custom-call | tf_op jit(solution)/shard_map/pallas_call | solution.py:449
  283.4 0.9 collective-permute-start
  284.3 1.8 collective-permute-start.1
  286.1 0.0 collective-permute-start.6
  286.1 2.7 collective-permute-start.8
  288.8 28.6 %shard_map.188 = (bf16[2,1024,3328]{2,1,0:T(8,128)(2,1)}, bf16[2,1024,3328]{2,1,0:T(8,128)(2,1)}, f32[2,128,3328]{2,1,0:T(8,128)}, f32[2,128,3328]{2,1,0:T(8,128...) custom-call(bf16[2,1024,3328]{2,1,0:T(8,128)(2,1)} %get-tuple-element., ...), custom_call_target="tpu_custom_call" | custom-call | tf_op jit(solution)/shard_map/pallas_call | solution.py:400
  317.4 0.0 collective-permute-done.refs_4_
  317.4 0.0 collective-permute-done.1.refs_5_
  317.4 0.1 collective-permute-start.10
  317.5 0.5 collective-permute-start.11
  318.0 0.1 collective-permute-start.4
  318.1 0.1 collective-permute-done.6.refs_6_
  318.2 0.3 collective-permute-start.5
  318.5 0.0 collective-permute-done.8.refs_7_
  318.5 0.2 collective-permute-start.7
  318.7 1.4 collective-permute-done.10.refs_6_
  320.1 0.1 collective-permute-start.9
  320.2 1.1 collective-permute-done.11.refs_7_
  321.3 0.0 collective-permute-start.3
  321.3 1.2 collective-permute-done.4.refs_2_
  322.5 1.5 collective-permute-start.2
  324.0 6.5 %shard_map.189 = (bf16[2,3328,1024]{2,1,0:T(8,128)(2,1)}, bf16[2,1024,3328]{2,1,0:T(8,128)(2,1)}) custom-call(bf16[2,1024,3328]{2,1,0:T(8,128)(2,1)} %get-tuple-element.116.refs_0_, bf16[2,208,1024]{2,1,0:T(8,128)(2,1)} %get-tuple-element.90.refs_1_, bf16[2,208,1024]{2,1,0:T(8,128)(2,1)} %get-tuple-element.91.refs_2_, ...), custom_call_target="tpu_custom_call", output_to_operand_aliasing={{1}: (0, {})} | custom-call | tf_op jit(solution)/shard_map/pallas_call | solution.py:374
  330.5 0.0 collective-permute-done.5.refs_3_
  330.5 0.0 collective-permute-done.7.refs_4_
  330.6 0.0 collective-permute-done.9.refs_5_
  330.6 0.0 copy-start.1
  330.6 0.0 copy-start
  330.6 2.4 shard_map.190
  333.0 10.1 %collective-permute-done.3.refs_1_ = bf16[2,208,1024]{2,1,0:T(8,128)(2,1)S(1)} collective-permute-done((bf16[2,208,1024]{2,1,0:T(8,128)(2,1)}, bf16[2,208,1024]{2,1,0:T(8,128)(2,1)S(1)}, u32[]{:S(2)}, u32[]{:S(2)}) %collective-permute-start.3) | collective-permute-done | bytes 852000 | tf_op jit(solution)/shard_map/ppermute | solution.py:429
  343.1 1.0 collective-permute-start.17
  344.1 0.0 collective-permute-done.2.refs_2_
  344.1 0.0 collective-permute-start.12
  344.1 0.0 copy-done.1
  344.1 0.1 collective-permute-start.13
  344.2 0.0 copy-done
  344.2 2.6 collective-permute-start.14
  346.8 1.2 shard_map.191.refs_0_
  348.1 1.4 collective-permute-done.13.refs_3_
  349.5 0.0 collective-permute-done.14.refs_4_
  349.5 1.3 collective-permute-start.15
  350.8 0.0 collective-permute-start.16
  350.8 0.0 collective-permute-done.17.refs_2_
  350.8 1.0 shard_map.192
  351.8 0.0 collective-permute-done.15.refs_3_
  351.8 0.3 collective-permute-done.16.refs_4_
  352.1 0.0 collective-permute-done.12.refs_2_
  352.1 1.0 shard_map.193
Async XLA Ops:
  283.4 34.0 %collective-permute-start = (bf16[2,208,1024]{2,1,0:T(8,128)(2,1)}, bf16[2,208,1024]{2,1,0:T(8,128)(2,1)}, u32[]{:S(2)}, u32[]{:S(2)}) collective-permute-start(bf16[2,208,1024]{2,1,0:T(8,128)(2,1)} %get-tuple-element.90.refs_1_), channel_id=1, source_target_pairs={{0,2},{1,3},{2,4},{3,5},{4,6},{5,7},{6,0},{7,1},{8,10},{9,11},{10,... | collective-permute-start | bytes 2555912 | tf_op jit(solution)/shard_map/ppermute | solution.py:429
  284.3 33.1 %collective-permute-start.1 = (bf16[2,208,1024]{2,1,0:T(8,128)(2,1)}, bf16[2,208,1024]{2,1,0:T(8,128)(2,1)}, u32[]{:S(2)}, u32[]{:S(2)}) collective-permute-start(bf16[2,208,1024]{2,1,0:T(8,128)(2,1)} %get-tuple-element.91.refs_2_), channel_id=1, source_target_pairs={{0,6},{1,7},{2,0},{3,1},{4,2},{5,3},{6,4},{7,5},{8,14},{9,15},{10,... | collective-permute-start | bytes 2555912 | tf_op jit(solution)/shard_map/ppermute | solution.py:429
  286.1 32.1 %collective-permute-start.6 = (bf16[2,208,1024]{2,1,0:T(8,128)(2,1)}, bf16[2,208,1024]{2,1,0:T(8,128)(2,1)}, u32[]{:S(2)}, u32[]{:S(2)}) collective-permute-start(bf16[2,208,1024]{2,1,0:T(8,128)(2,1)} %get-tuple-element.91.refs_2_), channel_id=1, source_target_pairs={{0,2},{1,3},{2,4},{3,5},{4,6},{5,7},{6,0},{7,1},{8,10},{9,11},{10,... | collective-permute-start | bytes 2555912 | tf_op jit(solution)/shard_map/ppermute | solution.py:429
  286.1 32.4 %collective-permute-start.8 = (bf16[2,208,1024]{2,1,0:T(8,128)(2,1)}, bf16[2,208,1024]{2,1,0:T(8,128)(2,1)}, u32[]{:S(2)}, u32[]{:S(2)}) collective-permute-start(bf16[2,208,1024]{2,1,0:T(8,128)(2,1)} %get-tuple-element.90.refs_1_), channel_id=1, source_target_pairs={{0,6},{1,7},{2,0},{3,1},{4,2},{5,3},{6,4},{7,5},{8,14},{9,15},{10,... | collective-permute-start | bytes 2555912 | tf_op jit(solution)/shard_map/ppermute | solution.py:429
  317.4 2.7 collective-permute-start.10
  317.5 3.8 %collective-permute-start.11 = (bf16[2,64,3328]{2,1,0:T(8,128)(2,1)}, bf16[2,64,3328]{2,1,0:T(8,128)(2,1)S(1)}, u32[]{:S(2)}, u32[]{:S(2)}) collective-permute-start(bf16[2,64,3328]{2,1,0:T(8,128)(2,1)} %get-tuple-element.115.refs_9_), channel_id=1, source_target_pairs={{0,1},{1,0},{2,3},{3,2},{4,5},{5,4},{6,7},{7,6},{8,9},{9,8},{10,11... | collective-permute-start | bytes 2555912 | tf_op jit(solution)/shard_map/ppermute | solution.py:432
  318.0 4.5 %collective-permute-start.4 = (bf16[2,208,1024]{2,1,0:T(8,128)(2,1)}, bf16[2,208,1024]{2,1,0:T(8,128)(2,1)S(1)}, u32[]{:S(2)}, u32[]{:S(2)}) collective-permute-start(bf16[2,208,1024]{2,1,0:T(8,128)(2,1)} %collective-permute-done.refs_4_), channel_id=1, source_target_pairs={{0,1},{1,0},{2,3},{3,2},{4,5},{5,4},{6,7},{7,6},{8,9},{9,8},{10,11... | collective-permute-start | bytes 2555912 | tf_op jit(solution)/shard_map/ppermute | solution.py:432
  318.2 12.3 %collective-permute-start.5 = (bf16[2,208,1024]{2,1,0:T(8,128)(2,1)}, bf16[2,208,1024]{2,1,0:T(8,128)(2,1)S(1)}, u32[]{:S(2)}, u32[]{:S(2)}) collective-permute-start(bf16[2,208,1024]{2,1,0:T(8,128)(2,1)} %collective-permute-done.1.refs_5_), channel_id=1, source_target_pairs={{0,1},{1,0},{2,3},{3,2},{4,5},{5,4},{6,7},{7,6},{8,9},{9,8},{10,11... | collective-permute-start | bytes 2555912 | tf_op jit(solution)/shard_map/ppermute | solution.py:432
  318.5 12.0 %collective-permute-start.7 = (bf16[2,208,1024]{2,1,0:T(8,128)(2,1)}, bf16[2,208,1024]{2,1,0:T(8,128)(2,1)S(1)}, u32[]{:S(2)}, u32[]{:S(2)}) collective-permute-start(bf16[2,208,1024]{2,1,0:T(8,128)(2,1)} %collective-permute-done.6.refs_6_), channel_id=1, source_target_pairs={{0,1},{1,0},{2,3},{3,2},{4,5},{5,4},{6,7},{7,6},{8,9},{9,8},{10,11... | collective-permute-start | bytes 2555912 | tf_op jit(solution)/shard_map/ppermute | solution.py:432
  320.1 10.5 %collective-permute-start.9 = (bf16[2,208,1024]{2,1,0:T(8,128)(2,1)}, bf16[2,208,1024]{2,1,0:T(8,128)(2,1)S(1)}, u32[]{:S(2)}, u32[]{:S(2)}) collective-permute-start(bf16[2,208,1024]{2,1,0:T(8,128)(2,1)} %collective-permute-done.8.refs_7_), channel_id=1, source_target_pairs={{0,1},{1,0},{2,3},{3,2},{4,5},{5,4},{6,7},{7,6},{8,9},{9,8},{10,11... | collective-permute-start | bytes 2555912 | tf_op jit(solution)/shard_map/ppermute | solution.py:432
  321.3 21.8 %collective-permute-start.3 = (bf16[2,208,1024]{2,1,0:T(8,128)(2,1)}, bf16[2,208,1024]{2,1,0:T(8,128)(2,1)S(1)}, u32[]{:S(2)}, u32[]{:S(2)}) collective-permute-start(bf16[2,208,1024]{2,1,0:T(8,128)(2,1)} %collective-permute-done.refs_4_), channel_id=1, source_target_pairs={{0,2},{1,3},{2,4},{3,5},{4,6},{5,7},{6,0},{7,1},{8,10},{9,11},{10,... | collective-permute-start | bytes 2555912 | tf_op jit(solution)/shard_map/ppermute | solution.py:429
  322.5 21.6 %collective-permute-start.2 = (bf16[2,208,1024]{2,1,0:T(8,128)(2,1)}, bf16[2,208,1024]{2,1,0:T(8,128)(2,1)S(1)}, u32[]{:S(2)}, u32[]{:S(2)}) collective-permute-start(bf16[2,208,1024]{2,1,0:T(8,128)(2,1)} %collective-permute-done.1.refs_5_), channel_id=1, source_target_pairs={{0,6},{1,7},{2,0},{3,1},{4,2},{5,3},{6,4},{7,5},{8,14},{9,15},{10,... | collective-permute-start | bytes 2555912 | tf_op jit(solution)/shard_map/ppermute | solution.py:429
  330.6 13.5 %copy-start.1 = (bf16[1,16,3328]{2,1,0:T(8,128)(2,1)S(1)}, bf16[1,16,3328]{2,1,0:T(8,128)(2,1)}, u32[]{:S(2)}) copy-start(bf16[1,16,3328]{2,1,0:T(8,128)(2,1)} %get-tuple-element.138) | copy-start | bytes 319492
  330.6 13.6 %copy-start = (bf16[1,16,3328]{2,1,0:T(8,128)(2,1)S(1)}, bf16[1,16,3328]{2,1,0:T(8,128)(2,1)}, u32[]{:S(2)}) copy-start(bf16[1,16,3328]{2,1,0:T(8,128)(2,1)} %get-tuple-element.139) | copy-start | bytes 319492
  343.1 7.7 %collective-permute-start.17 = (bf16[2,208,1024]{2,1,0:T(8,128)(2,1)S(1)}, bf16[2,208,1024]{2,1,0:T(8,128)(2,1)S(1)}, u32[]{:S(2)}, u32[]{:S(2)}) collective-permute-start(bf16[2,208,1024]{2,1,0:T(8,128)(2,1)S(1)} %collective-permute-done.3.refs_1_), channel_id=1, source_target_pairs={{0,1},{1,0},{2,3},{3,2},{4,5},{5,4},{6,7},{7,6},{8,9},{9,8},{10,11... | collective-permute-start | bytes 2555912 | tf_op jit(solution)/shard_map/ppermute | solution.py:432
  344.1 8.0 %collective-permute-start.12 = (bf16[2,208,1024]{2,1,0:T(8,128)(2,1)S(1)}, bf16[2,208,1024]{2,1,0:T(8,128)(2,1)S(1)}, u32[]{:S(2)}, u32[]{:S(2)}) collective-permute-start(bf16[2,208,1024]{2,1,0:T(8,128)(2,1)S(1)} %collective-permute-done.2.refs_2_), channel_id=1, source_target_pairs={{0,1},{1,0},{2,3},{3,2},{4,5},{5,4},{6,7},{7,6},{8,9},{9,8},{10,11... | collective-permute-start | bytes 2555912 | tf_op jit(solution)/shard_map/ppermute | solution.py:432
  344.1 5.4 %collective-permute-start.13 = (bf16[1,16,3328]{2,1,0:T(8,128)(2,1)S(1)}, bf16[1,16,3328]{2,1,0:T(8,128)(2,1)S(1)}, u32[]{:S(2)}, u32[]{:S(2)}) collective-permute-start(bf16[1,16,3328]{2,1,0:T(8,128)(2,1)S(1)} %copy-done.1), channel_id=1, source_target_pairs={{0,2},{1,3},{2,4},{3,5},{4,6},{5,7},{6,0},{7,1},{8,10},{9,11},{10,... | collective-permute-start | bytes 319496 | tf_op jit(solution)/shard_map/ppermute | solution.py:429
  344.2 5.3 %collective-permute-start.14 = (bf16[1,16,3328]{2,1,0:T(8,128)(2,1)S(1)}, bf16[1,16,3328]{2,1,0:T(8,128)(2,1)S(1)}, u32[]{:S(2)}, u32[]{:S(2)}) collective-permute-start(bf16[1,16,3328]{2,1,0:T(8,128)(2,1)S(1)} %copy-done), channel_id=1, source_target_pairs={{0,6},{1,7},{2,0},{3,1},{4,2},{5,3},{6,4},{7,5},{8,14},{9,15},{10,... | collective-permute-start | bytes 319496 | tf_op jit(solution)/shard_map/ppermute | solution.py:429
  349.5 2.3 collective-permute-start.15
  350.8 1.3 collective-permute-start.16
